TPU v7x, 32 devices: a whole 2x2x4 slice. The times are simulated.
32 devices in a mesh: inner: 2 (over y), outer: 4 (over z), head: 4 (over x, core).
Axes of the slice: x: 2, y: 2, z: 4, core: 2. Of those that a mesh axis runs over, the one named last changes fastest.
Arguments:
- queries: bfloat16 [2048, 64, 128], P(('inner', 'outer', 'head')), may hold values from -6 to 6
- key_vector_rows: bfloat16 [2048, 8, 128], P(('inner', 'outer'), 'head'), may hold values from -6 to 6
- value_vector_rows: bfloat16 [2048, 8, 128], P(('inner', 'outer'), 'head'), may hold values from -6 to 6
- grad_out: bfloat16 [2048, 64, 128], P(('inner', 'outer', 'head')), may hold values from -24 to 24
Outputs:
- query_grads: bfloat16 [2048, 64, 128], P(('inner', 'outer', 'head'))
- key_gradient_rows: bfloat16 [2048, 8, 128], P(('inner', 'outer'), 'head')
- value_gradient_rows: bfloat16 [2048, 8, 128], P(('inner', 'outer'), 'head')
All inputs are finite; a program needn't handle non-finite values.
Results may differ from a plain program's by a relative error of at most 0.012.
Values may be sent and summed in bfloat16 or wider, within the bound.
No kernel may reach another device: no remote copies, remote signals or barrier semaphores. Data moves between devices by JAX's collectives and lax.ppermute only.
A program may use at most 64 MiB of HBM per device.

v0:
```python
import jax
import jax.numpy as jnp
from jax import lax
from jax.sharding import PartitionSpec as P


def from_behind(value, axis, by):
    peers = lax.axis_size(axis)
    pairs = [(i, i + by) for i in range(peers) if 0 <= i + by < peers]
    return lax.ppermute(value, axis, pairs)


def head_grads(query_part, grad_part, key_part, value_part, allowed):
    softmax_scale = query_part.shape[-1] ** (-0.5)
    scores = (
        jnp.einsum("rgd,kd->grk", query_part, key_part, preferred_element_type=jnp.float32)
        * softmax_scale
    )
    scores = jnp.where(allowed[None], scores, -jnp.inf)
    highest = jnp.max(scores, axis=-1, keepdims=True)
    probs = jnp.exp(scores - highest)
    probs = probs / jnp.sum(probs, axis=-1, keepdims=True)
    probs_low = probs.astype(jnp.bfloat16)
    value_gradient_rows = jnp.einsum(
        "grk,rgd->kd", probs_low, grad_part, preferred_element_type=jnp.float32
    )
    dprobs = jnp.einsum("rgd,kd->grk", grad_part, value_part, preferred_element_type=jnp.float32)
    delta = jnp.sum(probs * dprobs, axis=-1, keepdims=True)
    dscores = (probs * (dprobs - delta)).astype(jnp.bfloat16)
    query_grads = (
        jnp.einsum("grk,kd->rgd", dscores, key_part, preferred_element_type=jnp.float32)
        * softmax_scale
    )
    key_gradient_rows = (
        jnp.einsum("grk,rgd->kd", dscores, query_part, preferred_element_type=jnp.float32)
        * softmax_scale
    )
    return (query_grads, key_gradient_rows, value_gradient_rows)


def block_grads(query_rows, grad_rows, key_window, value_window, allowed):
    row_count, head_count, width = query_rows.shape
    group_count = key_window.shape[1]
    heads_per_group = head_count // group_count
    query_split = query_rows.reshape(row_count, group_count, heads_per_group, width).transpose(
        1, 0, 2, 3
    )
    grad_split = grad_rows.reshape(row_count, group_count, heads_per_group, width).transpose(
        1, 0, 2, 3
    )
    key_split = key_window.transpose(1, 0, 2)
    value_split = value_window.transpose(1, 0, 2)
    query_grads, key_gradient_rows, value_gradient_rows = lax.map(
        lambda packed: head_grads(packed[0], packed[1], packed[2], packed[3], allowed),
        (query_split, grad_split, key_split, value_split),
    )
    query_grads = query_grads.transpose(1, 0, 2, 3).reshape(row_count, head_count, width)
    return (
        query_grads,
        key_gradient_rows.transpose(1, 0, 2),
        value_gradient_rows.transpose(1, 0, 2),
    )


def shards(queries, key_vector_rows, value_vector_rows, grad_out):
    tok_rows = key_vector_rows.shape[0]
    block_index = lax.axis_index(("inner", "outer"))
    query_rows, grad_rows = (
        lax.all_to_all(queries, "head", split_axis=1, concat_axis=0, tiled=True),
        lax.all_to_all(grad_out, "head", split_axis=1, concat_axis=0, tiled=True),
    )
    source = (key_vector_rows, value_vector_rows)
    query_positions = block_index * tok_rows + jnp.arange(tok_rows, dtype=jnp.int32)
    arrived = []
    for shift_by in (2, 1):
        arrived.append(from_behind((source[0], source[1]), ("inner", "outer"), shift_by))
    key_window = jnp.concatenate([arrived[0][0], arrived[1][0], source[0]], axis=0)
    value_window = jnp.concatenate([arrived[0][1], arrived[1][1], source[1]], axis=0)
    key_positions = (block_index - 2) * tok_rows + jnp.arange(3 * tok_rows, dtype=jnp.int32)
    allowed = (key_positions[None, :] <= query_positions[:, None]) & (key_positions[None, :] >= 0)
    query_grads, key_gradient_rows, value_gradient_rows = block_grads(
        query_rows, grad_rows, key_window, value_window, allowed
    )
    query_result = lax.all_to_all(
        query_grads.astype(jnp.bfloat16), "head", split_axis=0, concat_axis=1, tiled=True
    )
    key_slot_rows = key_gradient_rows.reshape(
        3, tok_rows, key_gradient_rows.shape[1], key_gradient_rows.shape[2]
    )
    value_slot_rows = value_gradient_rows.reshape(
        3, tok_rows, value_gradient_rows.shape[1], value_gradient_rows.shape[2]
    )
    key_total = key_slot_rows[2]
    value_total = value_slot_rows[2]
    for back_by in (1, 2):
        key_back, value_back = from_behind(
            (key_slot_rows[2 - back_by], value_slot_rows[2 - back_by]), ("inner", "outer"), -back_by
        )
        key_total = key_total + key_back
        value_total = value_total + value_back
    return (query_result, key_total.astype(jnp.bfloat16), value_total.astype(jnp.bfloat16))


def solution(mesh):
    return jax.shard_map(
        shards,
        mesh=mesh,
        in_specs=(
            P(("inner", "outer", "head"), None, None),
            P(("inner", "outer"), "head", None),
            P(("inner", "outer"), "head", None),
            P(("inner", "outer", "head"), None, None),
        ),
        out_specs=(
            P(("inner", "outer", "head"), None, None),
            P(("inner", "outer"), "head", None),
            P(("inner", "outer"), "head", None),
        ),
        check_vma=False,
    )
```

profile of v0, /device:TPU:0, one launch (start us, length us, event | category | flops | bytes accessed | tf_op | source)
XLA Modules:
  0.0 182.1 jit_solution(10710460803360977241)
XLA Ops:
  0.6 0.0 copy-start.8
  0.6 0.0 copy-start.9
  0.7 2.9 %copy.51 = bf16[64,64,128]{2,0,1:T(8,128)(2,1)} copy(bf16[64,64,128]{2,1,0:T(8,128)(2,1)} %param.6) | data formatting | bytes 2097152 | tf_op args[0]
  3.6 4.2 %all-to-all-start = ((bf16[64,64,128]{2,0,1:T(8,128)(2,1)}), bf16[64,64,128]{2,0,1:T(8,128)(2,1)S(1)}, u32[]{:S(2)}, u32[]{:S(2)}) async-start(bf16[64,64,128]{2,0,1:T(8,128)(2,1)} %copy.51), calls=%async_computation | async-start | bytes 2097152 | tf_op jit(solution)/shard_map/all_to_all | solution.py:69
  7.8 2.9 %copy.56 = bf16[64,64,128]{2,0,1:T(8,128)(2,1)} copy(bf16[64,64,128]{2,1,0:T(8,128)(2,1)} %param.9) | data formatting | bytes 2097152 | tf_op args[3]
  10.7 11.5 %all-to-all-done = bf16[64,64,128]{2,0,1:T(8,128)(2,1)S(1)} async-done(((bf16[64,64,128]{2,0,1:T(8,128)(2,1)}), bf16[64,64,128]{2,0,1:T(8,128)(2,1)S(1)}, u32[]{:S(2)}, u32[]{:S(2)}) %all-to-all-start) | async-done | bytes 1048608 | tf_op jit(solution)/shard_map/all_to_all | solution.py:69
  22.2 3.5 %all-to-all-start.1 = ((bf16[64,64,128]{2,0,1:T(8,128)(2,1)}), bf16[64,64,128]{2,0,1:T(8,128)(2,1)S(1)}, u32[]{:S(2)}, u32[]{:S(2)}) async-start(bf16[64,64,128]{2,0,1:T(8,128)(2,1)} %copy.56), calls=%async_computation.1 | async-start | bytes 2097152 | tf_op jit(solution)/shard_map/all_to_all | solution.py:70
  25.8 0.0 copy-done.8
  25.8 5.2 %collective-permute-start = (bf16[256,2,128]{2,0,1:T(8,128)(2,1)S(1)}, bf16[256,2,128]{2,0,1:T(8,128)(2,1)S(1)}, u32[]{:S(2)}, u32[]{:S(2)}) collective-permute-start(bf16[256,2,128]{2,0,1:T(8,128)(2,1)S(1)} %copy.48), channel_id=1, source_target_pairs={{0,8},{4,12},{8,16},{12,20},{16,24},{20,28},{1,9},{5,13},{9,17},{1... | collective-permute-start | bytes 393224 | tf_op jit(solution)/shard_map/ppermute | solution.py:10
  31.0 3.5 %collective-permute-start.1 = (bf16[256,2,128]{2,0,1:T(8,128)(2,1)S(1)}, bf16[256,2,128]{2,0,1:T(8,128)(2,1)S(1)}, u32[]{:S(2)}, u32[]{:S(2)}) collective-permute-start(bf16[256,2,128]{2,0,1:T(8,128)(2,1)S(1)} %copy.48), channel_id=1, source_target_pairs={{0,4},{4,8},{8,12},{12,16},{16,20},{20,24},{24,28},{1,5},{5,9},{9,... | collective-permute-start | bytes 393224 | tf_op jit(solution)/shard_map/ppermute | solution.py:10
  34.5 0.0 copy-done.9
  34.6 3.2 %collective-permute-start.2 = (bf16[256,2,128]{2,0,1:T(8,128)(2,1)S(1)}, bf16[256,2,128]{2,0,1:T(8,128)(2,1)S(1)}, u32[]{:S(2)}, u32[]{:S(2)}) collective-permute-start(bf16[256,2,128]{2,0,1:T(8,128)(2,1)S(1)} %copy.53), channel_id=1, source_target_pairs={{0,8},{4,12},{8,16},{12,20},{16,24},{20,28},{1,9},{5,13},{9,17},{1... | collective-permute-start | bytes 393224 | tf_op jit(solution)/shard_map/ppermute | solution.py:10
  37.8 4.4 %collective-permute-start.3 = (bf16[256,2,128]{2,0,1:T(8,128)(2,1)S(1)}, bf16[256,2,128]{2,0,1:T(8,128)(2,1)S(1)}, u32[]{:S(2)}, u32[]{:S(2)}) collective-permute-start(bf16[256,2,128]{2,0,1:T(8,128)(2,1)S(1)} %copy.53), channel_id=1, source_target_pairs={{0,4},{4,8},{8,12},{12,16},{16,20},{20,24},{24,28},{1,5},{5,9},{9,... | collective-permute-start | bytes 393224 | tf_op jit(solution)/shard_map/ppermute | solution.py:10
  42.2 0.6 iota_add_fusion.1
  42.8 0.0 collective-permute-done
  42.8 0.0 collective-permute-done.1
  42.8 0.8 maximum_bitcast_fusion
  43.6 0.0 collective-permute-done.2
  43.6 1.1 collective-permute-done.3
  44.7 0.1 copy.52
  44.8 0.0 all-to-all-done.1
  44.8 1.1 copy.57
  45.9 81.8 %while.15 = (s32[]{:T(128)}, bf16[2,256,8,128]{1,3,2,0:T(8,128)(2,1)}, f32[2,768,128]{2,0,1:T(2,128)}, f32[2,768,128]{2,0,1:T(2,128)}, bf16[2,768,128]{2,1,0:T(8...) while((s32[]{:T(128)}, ...), condition=%wide.region_4.5_spmd.clone, body=%wide.region_0.4_spmd.clone.sunk | while | flops 2034465536 | bytes 100918376 | solution.py:53
  45.9 1.1 compare_and_fusion.2
  47.0 5.7 %fusion.96 = (f32[8,256]{1,0:T(8,128)S(1)}, f32[8,256,768]{1,2,0:T(8,128)}) fusion(pred[256,768]{0,1:T(8,128)(4,1)S(1)} %compare_and_fusion.2, bf16[2,256,8,128]{3,1,2,0:T(8,128)(2,1)S(1)} %get-tuple-element.218, s32[]{:T(128)} %get-tuple-element.200, bf16[2,768,128]{2,1,0:T(8,128)(2,1)} %get-tuple-element.217), kind=kOutput, calls=%fused_computation.63.clone.1 | convolution fusion | flops 408945408 | bytes 7218176 | tf_op jit(solution)/shard_map/while/body/eval_jaxpr/sub | solution.py:21
  52.6 0.0 copy-done.3
  52.6 3.9 %fusion.97 = (f32[8,256]{1,0:T(8,128)S(1)}, f32[768,256,8]{1,0,2:T(8,128)S(1)}) fusion(f32[8,256,768]{1,2,0:T(8,128)} %get-tuple-element.183, f32[8,256]{1,0:T(8,128)S(1)} %get-tuple-element.184, bf16[2,256,8,128]{3,1,2,0:T(8,128)(2,1)S(1)} %copy-done.3, s32[]{:T(128)} %get-tuple-element.200, bf16[2,768,128]{2,1,0:T(8,128)(2,1)S(1)} %get-tuple-element.219), kind=kOutput, calls=%fused_computation.4.clone.1 | convolution fusion | flops 407369728 | bytes 13321216 | tf_op jit(solution)/shard_map/while/body/eval_jaxpr/rgd,kd->grk/dot_general | solution.py:27
  56.6 0.6 copy-done
  57.2 1.2 fusion.98
  58.4 2.0 %fusion.100 = f32[768,128]{1,0:T(8,128)S(1)} fusion(bf16[8,256,768]{1,2,0:T(8,128)(2,1)S(1)} %fusion.98, bf16[2,256,8,128]{3,1,2,0:T(8,128)(2,1)} %copy-done.1, s32[]{:T(128)} %get-tuple-element.200), kind=kOutput, calls=%fused_computation.20.clone.1 | convolution fusion | flops 402751488 | bytes 4063744 | tf_op jit(solution)/shard_map/while/body/eval_jaxpr/grk,rgd->kd/dot_general | solution.py:35
  60.4 10.6 %dynamic_update_slice.19 = f32[2,768,128]{2,0,1:T(2,128)} dynamic-update-slice(f32[2,768,128]{2,0,1:T(2,128)} %get-tuple-element.202, f32[1,768,128]{2,0,1:T(1,128)S(1)} %bitcast.141, s32[]{:T(128)} %get-tuple-element.200, s32[]{:T(128)} %constant.13.clone.1..sunk, s32[]{:T(128)} %constant.13.clone.1..sunk) | dynamic-update-slice | bytes 786436 | tf_op jit(solution)/shard_map/while/body/jit(dynamic_update_index_in_dim)/dynamic_update_slice | solution.py:53
  71.0 2.3 %fusion.99 = bf16[2,256,8,128]{1,3,2,0:T(8,128)(2,1)} fusion(bf16[2,256,8,128]{1,3,2,0:T(8,128)(2,1)} %get-tuple-element.201, s32[]{:T(128)} %get-tuple-element.200, bf16[8,256,768]{1,2,0:T(8,128)(2,1)S(1)} %fusion.98, bf16[2,768,128]{2,1,0:T(8,128)(2,1)} %get-tuple-element.217), kind=kOutput, calls=%fused_computation.18.clone.1 | convolution fusion | flops 402915328 | bytes 4391936 | tf_op jit(solution)/shard_map/while/body/eval_jaxpr/grk,kd->rgd/dot_general | solution.py:31
  73.3 4.0 %fusion.101 = f32[768,128,1]{1,0,2:T(8,128)S(1)} fusion(bf16[2,256,8,128]{3,1,2,0:T(8,128)(2,1)} %get-tuple-element.220, s32[]{:T(128)} %get-tuple-element.200, f32[8,256,768]{1,2,0:T(8,128)} %get-tuple-element.183, f32[8,256]{1,0:T(8,128)S(1)} %get-tuple-element.184), kind=kOutput, calls=%fused_computation.10.clone.1 | convolution fusion | flops 405798912 | bytes 7217664 | tf_op jit(solution)/shard_map/while/body/eval_jaxpr/grk,rgd->kd/dot_general | solution.py:24
  77.3 0.0 copy-done.4
  77.3 8.6 %dynamic_update_slice.20 = f32[2,768,128]{2,0,1:T(2,128)S(1)} dynamic-update-slice(f32[2,768,128]{2,0,1:T(2,128)S(1)} %copy-done.4, f32[1,768,128]{2,0,1:T(1,128)S(1)} %bitcast.143, s32[]{:T(128)} %get-tuple-element.200, s32[]{:T(128)} %constant.13.clone.1..sunk, s32[]{:T(128)} %constant.13.clone.1..sunk) | dynamic-update-slice | bytes 786436 | tf_op jit(solution)/shard_map/while/body/jit(dynamic_update_index_in_dim)/dynamic_update_slice | solution.py:53
  85.9 0.0 copy-start.5
  85.9 0.9 copy-done.5
  86.8 1.1 compare_and_fusion.2
  87.9 5.7 %fusion.96 = (f32[8,256]{1,0:T(8,128)S(1)}, f32[8,256,768]{1,2,0:T(8,128)}) fusion(pred[256,768]{0,1:T(8,128)(4,1)S(1)} %compare_and_fusion.2, bf16[2,256,8,128]{3,1,2,0:T(8,128)(2,1)S(1)} %get-tuple-element.218, s32[]{:T(128)} %get-tuple-element.200, bf16[2,768,128]{2,1,0:T(8,128)(2,1)} %get-tuple-element.217), kind=kOutput, calls=%fused_computation.63.clone.1 | convolution fusion | flops 408945408 | bytes 7218176 | tf_op jit(solution)/shard_map/while/body/eval_jaxpr/sub | solution.py:21
  93.5 3.9 %fusion.97 = (f32[8,256]{1,0:T(8,128)S(1)}, f32[768,256,8]{1,0,2:T(8,128)S(1)}) fusion(f32[8,256,768]{1,2,0:T(8,128)} %get-tuple-element.183, f32[8,256]{1,0:T(8,128)S(1)} %get-tuple-element.184, bf16[2,256,8,128]{3,1,2,0:T(8,128)(2,1)S(1)} %copy-done.3, s32[]{:T(128)} %get-tuple-element.200, bf16[2,768,128]{2,1,0:T(8,128)(2,1)S(1)} %get-tuple-element.219), kind=kOutput, calls=%fused_computation.4.clone.1 | convolution fusion | flops 407369728 | bytes 13321216 | tf_op jit(solution)/shard_map/while/body/eval_jaxpr/rgd,kd->grk/dot_general | solution.py:27
  97.5 0.6 copy-done
  98.1 1.2 fusion.98
  99.3 2.0 %fusion.100 = f32[768,128]{1,0:T(8,128)S(1)} fusion(bf16[8,256,768]{1,2,0:T(8,128)(2,1)S(1)} %fusion.98, bf16[2,256,8,128]{3,1,2,0:T(8,128)(2,1)} %copy-done.1, s32[]{:T(128)} %get-tuple-element.200), kind=kOutput, calls=%fused_computation.20.clone.1 | convolution fusion | flops 402751488 | bytes 4063744 | tf_op jit(solution)/shard_map/while/body/eval_jaxpr/grk,rgd->kd/dot_general | solution.py:35
  101.3 10.6 %dynamic_update_slice.19 = f32[2,768,128]{2,0,1:T(2,128)} dynamic-update-slice(f32[2,768,128]{2,0,1:T(2,128)} %get-tuple-element.202, f32[1,768,128]{2,0,1:T(1,128)S(1)} %bitcast.141, s32[]{:T(128)} %get-tuple-element.200, s32[]{:T(128)} %constant.13.clone.1..sunk, s32[]{:T(128)} %constant.13.clone.1..sunk) | dynamic-update-slice | bytes 786436 | tf_op jit(solution)/shard_map/while/body/jit(dynamic_update_index_in_dim)/dynamic_update_slice | solution.py:53
  111.9 2.3 %fusion.99 = bf16[2,256,8,128]{1,3,2,0:T(8,128)(2,1)} fusion(bf16[2,256,8,128]{1,3,2,0:T(8,128)(2,1)} %get-tuple-element.201, s32[]{:T(128)} %get-tuple-element.200, bf16[8,256,768]{1,2,0:T(8,128)(2,1)S(1)} %fusion.98, bf16[2,768,128]{2,1,0:T(8,128)(2,1)} %get-tuple-element.217), kind=kOutput, calls=%fused_computation.18.clone.1 | convolution fusion | flops 402915328 | bytes 4391936 | tf_op jit(solution)/shard_map/while/body/eval_jaxpr/grk,kd->rgd/dot_general | solution.py:31
  114.2 4.0 %fusion.101 = f32[768,128,1]{1,0,2:T(8,128)S(1)} fusion(bf16[2,256,8,128]{3,1,2,0:T(8,128)(2,1)} %get-tuple-element.220, s32[]{:T(128)} %get-tuple-element.200, f32[8,256,768]{1,2,0:T(8,128)} %get-tuple-element.183, f32[8,256]{1,0:T(8,128)S(1)} %get-tuple-element.184), kind=kOutput, calls=%fused_computation.10.clone.1 | convolution fusion | flops 405798912 | bytes 7217664 | tf_op jit(solution)/shard_map/while/body/eval_jaxpr/grk,rgd->kd/dot_general | solution.py:24
  118.2 8.6 %dynamic_update_slice.20 = f32[2,768,128]{2,0,1:T(2,128)S(1)} dynamic-update-slice(f32[2,768,128]{2,0,1:T(2,128)S(1)} %copy-done.4, f32[1,768,128]{2,0,1:T(1,128)S(1)} %bitcast.143, s32[]{:T(128)} %get-tuple-element.200, s32[]{:T(128)} %constant.13.clone.1..sunk, s32[]{:T(128)} %constant.13.clone.1..sunk) | dynamic-update-slice | bytes 786436 | tf_op jit(solution)/shard_map/while/body/jit(dynamic_update_index_in_dim)/dynamic_update_slice | solution.py:53
  126.8 0.9 copy-done.5
  127.6 2.6 %copy.58 = bf16[256,2,8,128]{3,2,1,0:T(8,128)(2,1)} copy(bf16[256,2,8,128]{0,3,2,1:T(8,128)(2,1)} %bitcast.148) | data formatting | bytes 2097152 | tf_op jit(solution)/shard_map/convert_element_type | solution.py:85
  130.3 3.5 %all-to-all-start.2 = ((bf16[256,16,128]{2,1,0:T(8,128)(2,1)}), bf16[256,16,128]{2,1,0:T(8,128)(2,1)S(1)}, u32[]{:S(2)}, u32[]{:S(2)}) async-start(bf16[256,16,128]{2,1,0:T(8,128)(2,1)} %bitcast.11), calls=%async_computation.2 | async-start | bytes 2097152 | tf_op jit(solution)/shard_map/all_to_all | solution.py:84
  133.8 1.1 fusion.70
  134.9 1.3 collective-permute-start.6
  136.2 1.3 collective-permute-start.7
  137.5 1.1 fusion.71
  138.5 1.3 collective-permute-start.4
  139.8 1.3 collective-permute-start.5
  141.1 8.1 %collective-permute-done.6 = f32[256,2,128]{2,1,0:T(2,128)S(1)} collective-permute-done((f32[256,2,128]{2,1,0:T(2,128)S(1)}, f32[256,2,128]{2,1,0:T(2,128)S(1)}, u32[]{:S(2)}, u32[]{:S(2)}) %collective-permute-start.6) | collective-permute-done | bytes 262176 | tf_op jit(solution)/shard_map/ppermute | solution.py:10
  149.2 13.1 %collective-permute-done.7 = f32[256,2,128]{2,1,0:T(2,128)S(1)} collective-permute-done((f32[256,2,128]{2,1,0:T(2,128)S(1)}, f32[256,2,128]{2,1,0:T(2,128)S(1)}, u32[]{:S(2)}, u32[]{:S(2)}) %collective-permute-start.7) | collective-permute-done | bytes 262176 | tf_op jit(solution)/shard_map/ppermute | solution.py:10
  162.3 1.8 fusion.58
  164.1 0.0 collective-permute-done.4
  164.1 14.8 %collective-permute-done.5 = f32[256,2,128]{2,1,0:T(2,128)S(1)} collective-permute-done((f32[256,2,128]{2,1,0:T(2,128)S(1)}, f32[256,2,128]{2,1,0:T(2,128)S(1)}, u32[]{:S(2)}, u32[]{:S(2)}) %collective-permute-start.5) | collective-permute-done | bytes 262176 | tf_op jit(solution)/shard_map/ppermute | solution.py:10
  179.0 1.8 fusion.60
  180.8 0.0 all-to-all-done.2
  180.8 1.3 copy.59
  (33 shorter events, 0.1 us)
Async XLA Ops:
  0.6 25.1 %copy-start.8 = (bf16[256,2,128]{2,1,0:T(2,128)(2,1)S(1)}, bf16[256,2,128]{2,1,0:T(2,128)(2,1)}, u32[]{:S(2)}) copy-start(bf16[256,2,128]{2,1,0:T(2,128)(2,1)} %param.7) | copy-start | bytes 393220
  0.6 33.9 %copy-start.9 = (bf16[256,2,128]{2,1,0:T(2,128)(2,1)S(1)}, bf16[256,2,128]{2,1,0:T(2,128)(2,1)}, u32[]{:S(2)}) copy-start(bf16[256,2,128]{2,1,0:T(2,128)(2,1)} %param.8) | copy-start | bytes 393220
  3.6 18.7 %all-to-all-start = ((bf16[64,64,128]{2,0,1:T(8,128)(2,1)}), bf16[64,64,128]{2,0,1:T(8,128)(2,1)S(1)}, u32[]{:S(2)}, u32[]{:S(2)}) async-start(bf16[64,64,128]{2,0,1:T(8,128)(2,1)} %copy.51), calls=%async_computation | async-start | bytes 2097152 | tf_op jit(solution)/shard_map/all_to_all | solution.py:69
  22.2 22.6 %all-to-all-start.1 = ((bf16[64,64,128]{2,0,1:T(8,128)(2,1)}), bf16[64,64,128]{2,0,1:T(8,128)(2,1)S(1)}, u32[]{:S(2)}, u32[]{:S(2)}) async-start(bf16[64,64,128]{2,0,1:T(8,128)(2,1)} %copy.56), calls=%async_computation.1 | async-start | bytes 2097152 | tf_op jit(solution)/shard_map/all_to_all | solution.py:70
  25.8 17.0 %collective-permute-start = (bf16[256,2,128]{2,0,1:T(8,128)(2,1)S(1)}, bf16[256,2,128]{2,0,1:T(8,128)(2,1)S(1)}, u32[]{:S(2)}, u32[]{:S(2)}) collective-permute-start(bf16[256,2,128]{2,0,1:T(8,128)(2,1)S(1)} %copy.48), channel_id=1, source_target_pairs={{0,8},{4,12},{8,16},{12,20},{16,24},{20,28},{1,9},{5,13},{9,17},{1... | collective-permute-start | bytes 393224 | tf_op jit(solution)/shard_map/ppermute | solution.py:10
  31.0 11.7 %collective-permute-start.1 = (bf16[256,2,128]{2,0,1:T(8,128)(2,1)S(1)}, bf16[256,2,128]{2,0,1:T(8,128)(2,1)S(1)}, u32[]{:S(2)}, u32[]{:S(2)}) collective-permute-start(bf16[256,2,128]{2,0,1:T(8,128)(2,1)S(1)} %copy.48), channel_id=1, source_target_pairs={{0,4},{4,8},{8,12},{12,16},{16,20},{20,24},{24,28},{1,5},{5,9},{9,... | collective-permute-start | bytes 393224 | tf_op jit(solution)/shard_map/ppermute | solution.py:10
  34.6 9.0 %collective-permute-start.2 = (bf16[256,2,128]{2,0,1:T(8,128)(2,1)S(1)}, bf16[256,2,128]{2,0,1:T(8,128)(2,1)S(1)}, u32[]{:S(2)}, u32[]{:S(2)}) collective-permute-start(bf16[256,2,128]{2,0,1:T(8,128)(2,1)S(1)} %copy.53), channel_id=1, source_target_pairs={{0,8},{4,12},{8,16},{12,20},{16,24},{20,28},{1,9},{5,13},{9,17},{1... | collective-permute-start | bytes 393224 | tf_op jit(solution)/shard_map/ppermute | solution.py:10
  37.8 6.9 %collective-permute-start.3 = (bf16[256,2,128]{2,0,1:T(8,128)(2,1)S(1)}, bf16[256,2,128]{2,0,1:T(8,128)(2,1)S(1)}, u32[]{:S(2)}, u32[]{:S(2)}) collective-permute-start(bf16[256,2,128]{2,0,1:T(8,128)(2,1)S(1)} %copy.53), channel_id=1, source_target_pairs={{0,4},{4,8},{8,12},{12,16},{16,20},{20,24},{24,28},{1,5},{5,9},{9,... | collective-permute-start | bytes 393224 | tf_op jit(solution)/shard_map/ppermute | solution.py:10
  45.9 10.7 %copy-start.1 = (bf16[2,256,8,128]{3,1,2,0:T(8,128)(2,1)}, bf16[2,256,8,128]{3,1,2,0:T(8,128)(2,1)S(1)}, u32[]{:S(2)}) copy-start(bf16[2,256,8,128]{3,1,2,0:T(8,128)(2,1)S(1)} %get-tuple-element.218) | copy-start | bytes 3145732 | tf_op jit(solution)/shard_map/while
  45.9 10.7 %copy-start.6 = (bf16[2,768,128]{2,1,0:T(8,128)(2,1)}, bf16[2,768,128]{2,1,0:T(8,128)(2,1)S(1)}, u32[]{:S(2)}) copy-start(bf16[2,768,128]{2,1,0:T(8,128)(2,1)S(1)} %get-tuple-element.219) | copy-start | bytes 1179652 | tf_op jit(solution)/shard_map/while
  45.9 6.7 %copy-start.3 = (bf16[2,256,8,128]{3,1,2,0:T(8,128)(2,1)S(1)}, bf16[2,256,8,128]{3,1,2,0:T(8,128)(2,1)}, u32[]{:S(2)}) copy-start(bf16[2,256,8,128]{3,1,2,0:T(8,128)(2,1)} %get-tuple-element.220) | copy-start | bytes 3145732 | tf_op jit(solution)/shard_map/while
  52.6 4.6 %copy-start = (f32[8,256,768]{1,2,0:T(8,128)S(1)}, f32[8,256,768]{1,2,0:T(8,128)}, u32[]{:S(2)}) copy-start(f32[8,256,768]{1,2,0:T(8,128)} %get-tuple-element.183) | copy-start | bytes 18874372 | tf_op jit(solution)/shard_map/while
  73.3 4.0 %copy-start.4 = (f32[2,768,128]{2,0,1:T(2,128)S(1)}, f32[2,768,128]{2,0,1:T(2,128)}, u32[]{:S(2)}) copy-start(f32[2,768,128]{2,0,1:T(2,128)} %get-tuple-element.203) | copy-start | bytes 2359300 | tf_op jit(solution)/shard_map/while
  73.3 13.4 %copy-start.2 = (bf16[2,256,8,128]{3,1,2,0:T(8,128)(2,1)S(1)}, bf16[2,256,8,128]{3,1,2,0:T(8,128)(2,1)}, u32[]{:S(2)}) copy-start(bf16[2,256,8,128]{3,1,2,0:T(8,128)(2,1)} %copy-done.1) | copy-start | bytes 3145732 | tf_op jit(solution)/shard_map/while
  73.3 13.4 %copy-start.7 = (bf16[2,768,128]{2,1,0:T(8,128)(2,1)S(1)}, bf16[2,768,128]{2,1,0:T(8,128)(2,1)}, u32[]{:S(2)}) copy-start(bf16[2,768,128]{2,1,0:T(8,128)(2,1)} %copy-done.6) | copy-start | bytes 1179652 | tf_op jit(solution)/shard_map/while
  85.9 0.9 copy-start.5
  86.8 10.7 %copy-start.1 = (bf16[2,256,8,128]{3,1,2,0:T(8,128)(2,1)}, bf16[2,256,8,128]{3,1,2,0:T(8,128)(2,1)S(1)}, u32[]{:S(2)}) copy-start(bf16[2,256,8,128]{3,1,2,0:T(8,128)(2,1)S(1)} %get-tuple-element.218) | copy-start | bytes 3145732 | tf_op jit(solution)/shard_map/while
  86.8 10.7 %copy-start.6 = (bf16[2,768,128]{2,1,0:T(8,128)(2,1)}, bf16[2,768,128]{2,1,0:T(8,128)(2,1)S(1)}, u32[]{:S(2)}) copy-start(bf16[2,768,128]{2,1,0:T(8,128)(2,1)S(1)} %get-tuple-element.219) | copy-start | bytes 1179652 | tf_op jit(solution)/shard_map/while
  86.8 6.7 %copy-start.3 = (bf16[2,256,8,128]{3,1,2,0:T(8,128)(2,1)S(1)}, bf16[2,256,8,128]{3,1,2,0:T(8,128)(2,1)}, u32[]{:S(2)}) copy-start(bf16[2,256,8,128]{3,1,2,0:T(8,128)(2,1)} %get-tuple-element.220) | copy-start | bytes 3145732 | tf_op jit(solution)/shard_map/while
  93.5 4.6 %copy-start = (f32[8,256,768]{1,2,0:T(8,128)S(1)}, f32[8,256,768]{1,2,0:T(8,128)}, u32[]{:S(2)}) copy-start(f32[8,256,768]{1,2,0:T(8,128)} %get-tuple-element.183) | copy-start | bytes 18874372 | tf_op jit(solution)/shard_map/while
  114.2 4.0 %copy-start.4 = (f32[2,768,128]{2,0,1:T(2,128)S(1)}, f32[2,768,128]{2,0,1:T(2,128)}, u32[]{:S(2)}) copy-start(f32[2,768,128]{2,0,1:T(2,128)} %get-tuple-element.203) | copy-start | bytes 2359300 | tf_op jit(solution)/shard_map/while
  114.2 13.4 %copy-start.2 = (bf16[2,256,8,128]{3,1,2,0:T(8,128)(2,1)S(1)}, bf16[2,256,8,128]{3,1,2,0:T(8,128)(2,1)}, u32[]{:S(2)}) copy-start(bf16[2,256,8,128]{3,1,2,0:T(8,128)(2,1)} %copy-done.1) | copy-start | bytes 3145732 | tf_op jit(solution)/shard_map/while
  114.2 13.4 %copy-start.7 = (bf16[2,768,128]{2,1,0:T(8,128)(2,1)S(1)}, bf16[2,768,128]{2,1,0:T(8,128)(2,1)}, u32[]{:S(2)}) copy-start(bf16[2,768,128]{2,1,0:T(8,128)(2,1)} %copy-done.6) | copy-start | bytes 1179652 | tf_op jit(solution)/shard_map/while
  126.8 0.9 copy-start.5
  130.3 50.5 %all-to-all-start.2 = ((bf16[256,16,128]{2,1,0:T(8,128)(2,1)}), bf16[256,16,128]{2,1,0:T(8,128)(2,1)S(1)}, u32[]{:S(2)}, u32[]{:S(2)}) async-start(bf16[256,16,128]{2,1,0:T(8,128)(2,1)} %bitcast.11), calls=%async_computation.2 | async-start | bytes 2097152 | tf_op jit(solution)/shard_map/all_to_all | solution.py:84
  134.9 14.3 %collective-permute-start.6 = (f32[256,2,128]{2,1,0:T(2,128)S(1)}, f32[256,2,128]{2,1,0:T(2,128)S(1)}, u32[]{:S(2)}, u32[]{:S(2)}) collective-permute-start(f32[256,2,128]{2,1,0:T(2,128)S(1)} %get-tuple-element.108), channel_id=1, source_target_pairs={{4,0},{8,4},{12,8},{16,12},{20,16},{24,20},{28,24},{5,1},{9,5},{13... | collective-permute-start | bytes 786440 | tf_op jit(solution)/shard_map/ppermute | solution.py:10
  136.2 26.2 %collective-permute-start.7 = (f32[256,2,128]{2,1,0:T(2,128)S(1)}, f32[256,2,128]{2,1,0:T(2,128)S(1)}, u32[]{:S(2)}, u32[]{:S(2)}) collective-permute-start(f32[256,2,128]{2,1,0:T(2,128)S(1)} %get-tuple-element.109), channel_id=1, source_target_pairs={{8,0},{12,4},{16,8},{20,12},{24,16},{28,20},{9,1},{13,5},{17,9},{2... | collective-permute-start | bytes 786440 | tf_op jit(solution)/shard_map/ppermute | solution.py:10
  138.5 25.6 %collective-permute-start.4 = (f32[256,2,128]{2,1,0:T(2,128)S(1)}, f32[256,2,128]{2,1,0:T(2,128)S(1)}, u32[]{:S(2)}, u32[]{:S(2)}) collective-permute-start(f32[256,2,128]{2,1,0:T(2,128)S(1)} %get-tuple-element.110), channel_id=1, source_target_pairs={{4,0},{8,4},{12,8},{16,12},{20,16},{24,20},{28,24},{5,1},{9,5},{13... | collective-permute-start | bytes 786440 | tf_op jit(solution)/shard_map/ppermute | solution.py:10
  139.8 39.1 %collective-permute-start.5 = (f32[256,2,128]{2,1,0:T(2,128)S(1)}, f32[256,2,128]{2,1,0:T(2,128)S(1)}, u32[]{:S(2)}, u32[]{:S(2)}) collective-permute-start(f32[256,2,128]{2,1,0:T(2,128)S(1)} %get-tuple-element.111), channel_id=1, source_target_pairs={{8,0},{12,4},{16,8},{20,12},{24,16},{28,20},{9,1},{13,5},{17,9},{2... | collective-permute-start | bytes 786440 | tf_op jit(solution)/shard_map/ppermute | solution.py:10
where the time goes:
time: 184 us; the launch traced here: 182 us
  local copies, waits for them, and re-layouts  54.4 us (30%)
  waiting for transfers between devices  48.7 us (26%)
  matrix products  35.8 us (19%)
  starting transfers between devices  32.7 us (18%)
  other arithmetic  9.45 us (5%)
    dynamic_update_slice x4, local copies, waits for them, and re-layouts, block_grads(): lax.map(lambda packed: head_grads(packed[0], packed[1], packed[2], packed...  38.2 us
    ppermute x8, waiting for transfers between devices, from_behind(): return lax.ppermute(value, axis, pairs)  37.1 us
    ppermute x8, starting transfers between devices, from_behind(): return lax.ppermute(value, axis, pairs)  21.5 us
    all_to_all x1, waiting for transfers between devices, shards(): lax.all_to_all(queries, 'head', split_axis=1, concat_axis=0, tiled=True)  11.5 us
    sub x2, matrix products, head_grads(): probs = jnp.exp(scores - highest)  11.3 us
    dot_general x2, matrix products, head_grads(): jnp.einsum('grk,rgd->kd', probs_low, grad_part, preferred_element_type=jn...  7.94 us
    dot_general x2, matrix products, head_grads(): jnp.einsum('rgd,kd->grk', grad_part, value_part, preferred_element_type=j...  7.84 us
    unnamed x8, local copies, waits for them, and re-layouts  5.86 us
  transfers between devices with their start and end apart: 11, of which 5 were waited for; matrix products, arithmetic and copies ran while one was open for 6% of the time, Pallas kernels for 0%

commit v1 on v0

v1 whole, which is shorter than its diff:
```python
import functools
import math

import jax
import jax.numpy as jnp
from jax import lax
from jax.experimental import pallas as pl
from jax.experimental.pallas import tpu as pltpu
from jax.sharding import PartitionSpec as P

NT = (((1,), (1,)), ((), ()))
SEQ = ("inner", "outer")
NEVER = 1e30


def shifted(value, by):
    peers = lax.axis_size(SEQ)
    pairs = [(i, i + by) for i in range(peers) if 0 <= i + by < peers]
    return lax.ppermute(value, SEQ, pairs)


def grads_kernel(
    group, bias_ref, q_ref, do_ref, far_ref, near_ref, own_ref,
    dq_ref, dfar_ref, dnear_ref, down_ref, acc, kt,
):
    step = pl.program_id(1)
    rows, width = q_ref.shape
    tok_rows = own_ref.shape[1]
    scale = width ** (-0.5)
    to_exp2 = scale * math.log2(math.e)
    windows = (far_ref, near_ref, own_ref)

    @pl.when(step == 0)
    def _():
        acc[...] = jnp.zeros_like(acc)
        for j, window in enumerate(windows):
            kt[j] = window[0].T

    q = q_ref[...]
    do = do_ref[...]
    bias = (bias_ref[0], bias_ref[1], 0.0)
    scores, tops = [], []
    for j, window in enumerate(windows):
        s = lax.dot_general(window[0], q, NT, preferred_element_type=jnp.float32)
        if j == 2:
            token = (lax.broadcasted_iota(jnp.int32, s.shape, 1) + step * rows) // group
            key = lax.broadcasted_iota(jnp.int32, s.shape, 0)
            s = jnp.where(key <= token, s, -jnp.inf)
        scores.append(s)
        tops.append(jnp.max(s, axis=0, keepdims=True) - bias[j])
    top = jnp.maximum(jnp.maximum(tops[0], tops[1]), tops[2]) * to_exp2
    weights, dprobs, total, dtotal = [], [], 0.0, 0.0
    for j, window in enumerate(windows):
        e = jnp.exp2(scores[j] * to_exp2 - (top + bias[j]))
        dp = lax.dot_general(window[1], do, NT, preferred_element_type=jnp.float32)
        total = total + jnp.sum(e, axis=0, keepdims=True)
        dtotal = dtotal + jnp.sum(e * dp, axis=0, keepdims=True)
        weights.append(e)
        dprobs.append(dp)
    inverse = 1.0 / total
    delta = dtotal * inverse
    dqt = 0.0
    for j in range(3):
        p = weights[j] * inverse
        ds = (p * (dprobs[j] - delta)).astype(jnp.bfloat16)
        acc[j, 1] += jnp.dot(p.astype(jnp.bfloat16), do, preferred_element_type=jnp.float32)
        acc[j, 0] += jnp.dot(ds, q, preferred_element_type=jnp.float32)
        dqt = dqt + jnp.dot(kt[j], ds, preferred_element_type=jnp.float32)
    dq_ref[...] = (dqt * scale).T.astype(dq_ref.dtype)

    @pl.when(step == pl.num_programs(1) - 1)
    def _():
        for j, out in enumerate((dfar_ref, dnear_ref, down_ref)):
            out[0] = (acc[j, 0] * scale).astype(out.dtype)
            out[1] = acc[j, 1].astype(out.dtype)


def group_grads(bias, pairs, far, near, own, group):
    sources, kv_heads, _, rows, width = pairs.shape
    tok_rows = own.shape[2]
    window = pl.BlockSpec((None, 2, tok_rows, width), lambda h, i: (h, 0, 0, 0))

    def half(which):
        return pl.BlockSpec((None, None, None, rows, width), lambda h, i: (i, h, which, 0, 0))

    shape = (kv_heads, 2, tok_rows, width)
    steps = kv_heads * sources * rows * 3 * tok_rows
    return pl.pallas_call(
        functools.partial(grads_kernel, group),
        grid=(kv_heads, sources),
        in_specs=[pl.BlockSpec(memory_space=pltpu.SMEM), half(0), half(1), window, window, window],
        out_specs=[
            pl.BlockSpec((None, None, rows, width), lambda h, i: (i, h, 0, 0)),
            window, window, window,
        ],
        out_shape=[
            jax.ShapeDtypeStruct((sources, kv_heads, rows, width), jnp.bfloat16),
            jax.ShapeDtypeStruct(shape, jnp.bfloat16),
            jax.ShapeDtypeStruct(shape, jnp.bfloat16),
            jax.ShapeDtypeStruct(shape, jnp.float32),
        ],
        scratch_shapes=[
            pltpu.VMEM((3, 2, tok_rows, width), jnp.float32),
            pltpu.VMEM((3, width, tok_rows), jnp.bfloat16),
        ],
        compiler_params=pltpu.CompilerParams(dimension_semantics=("arbitrary", "arbitrary")),
        cost_estimate=pl.CostEstimate(
            flops=10 * steps * width, bytes_accessed=8 * sources * rows * width, transcendentals=steps
        ),
        name="grads",
    )(bias, pairs, pairs, far, near, own)


def shards(queries, key_vector_rows, value_vector_rows, grad_out):
    part_rows, heads, width = queries.shape
    tok_rows, kv_heads, _ = key_vector_rows.shape
    peers = lax.axis_size("head")
    group = heads // (peers * kv_heads)
    block_index = lax.axis_index(SEQ)
    bias = jnp.where(block_index < jnp.array([2, 1]), NEVER, 0.0).astype(jnp.float32)

    def by_peer(value):
        return value.reshape(part_rows, peers, kv_heads, group, width).transpose(1, 2, 0, 3, 4)

    pairs = jnp.stack([by_peer(queries), by_peer(grad_out)], axis=2)
    pairs = pairs.reshape(peers, kv_heads, 2, part_rows * group, width)
    pairs = lax.all_to_all(pairs, "head", split_axis=0, concat_axis=0, tiled=True)
    own = jnp.stack([key_vector_rows.transpose(1, 0, 2), value_vector_rows.transpose(1, 0, 2)], axis=1)
    far = shifted(own, 2)
    near = shifted(own, 1)
    dq, dfar, dnear, down = group_grads(bias, pairs, far, near, own, group)
    dq = lax.all_to_all(dq, "head", split_axis=0, concat_axis=0, tiled=True)
    dq = dq.reshape(peers, kv_heads, part_rows, group, width).transpose(2, 0, 1, 3, 4)
    total = down + shifted(dnear, -1).astype(jnp.float32) + shifted(dfar, -2).astype(jnp.float32)
    total = total.astype(jnp.bfloat16).transpose(1, 2, 0, 3)
    return dq.reshape(part_rows, heads, width), total[0], total[1]


def solution(mesh):
    return jax.shard_map(
        shards,
        mesh=mesh,
        in_specs=(
            P(("inner", "outer", "head"), None, None),
            P(("inner", "outer"), "head", None),
            P(("inner", "outer"), "head", None),
            P(("inner", "outer", "head"), None, None),
        ),
        out_specs=(
            P(("inner", "outer", "head"), None, None),
            P(("inner", "outer"), "head", None),
            P(("inner", "outer"), "head", None),
        ),
        check_vma=False,
    )
```

time: 184 us -> 82.8 us (0.45)
  the two profiles are of different devices: /device:TPU:0 before, /device:TPU:27 now
where the time goes in v1:
time: 82.8 us; the launch traced here: 82.4 us
  waiting for transfers between devices  35.2 us (43%)
  starting transfers between devices  21 us (25%)
  Pallas kernels  17 us (21%)
  local copies, waits for them, and re-layouts  6.31 us (8%)
  other arithmetic  2.16 us (3%)
    ppermute x4, waiting for transfers between devices, shifted(): return lax.ppermute(value, SEQ, pairs)  29 us
    pallas_call x1, Pallas kernels, group_grads(): pl.pallas_call(functools.partial(grads_kernel, group), grid=(kv_heads, so...  17 us
    ppermute x4, starting transfers between devices, shifted(): return lax.ppermute(value, SEQ, pairs)  11 us
    all_to_all x1, waiting for transfers between devices, shards(): lax.all_to_all(pairs, 'head', split_axis=0, concat_axis=0, tiled=True)  6.2 us
    all_to_all x1, starting transfers between devices, shards(): dq = lax.all_to_all(dq, 'head', split_axis=0, concat_axis=0, tiled=True)  5.48 us
    all_to_all x1, starting transfers between devices, shards(): lax.all_to_all(pairs, 'head', split_axis=0, concat_axis=0, tiled=True)  4.53 us
    unnamed x22, local copies, waits for them, and re-layouts  2.94 us
    another operation x1, local copies, waits for them, and re-layouts, shards(): pairs = jnp.stack([by_peer(queries), by_peer(grad_out)], axis=2)  2.05 us
  transfers between devices with their start and end apart: 6, of which 4 were waited for; matrix products, arithmetic and copies ran while one was open for 3% of the time, Pallas kernels for 0%

profile of v1, /device:TPU:27, one launch (start us, length us, event | category | flops | bytes accessed | tf_op | source)
XLA Modules:
  0.0 82.4 jit_solution(7930849008400883060)
XLA Ops:
  0.6 2.0 %copy_bitcast_fusion = (bf16[4,2,1,512,128]{4,3,2,1,0:T(8,128)(2,1)S(1)}, bf16[4,2,1,512,128]{4,3,2,1,0:T(8,128)(2,1)S(1)}) fusion(bf16[64,4,2,8,128]{4,3,2,1,0:T(8,128)(2,1)} %bitcast.30, bf16[64,4,2,8,128]{4,3,2,1,0:T(8,128)(2,1)} %bitcast.31), kind=kLoop, calls=%fused_computation.1 | loop fusion | bytes 4194304 | tf_op jit(solution)/shard_map/stack | solution.py:125
  2.7 1.5 %pad_maximum_fusion = bf16[4,2,2,512,128]{4,3,2,1,0:T(8,128)(2,1)} fusion(bf16[4,2,1,512,128]{4,3,2,1,0:T(8,128)(2,1)S(1)} %get-tuple-element.16, bf16[4,2,1,512,128]{4,3,2,1,0:T(8,128)(2,1)S(1)} %get-tuple-element.17), kind=kLoop, calls=%fused_computation | loop fusion | flops 1048576 | bytes 4194304 | tf_op jit(solution)/shard_map/stack | solution.py:125
  4.2 0.0 copy-start.3
  4.2 0.0 copy-start.4
  4.2 0.0 copy-start.9
  4.2 4.5 %all-to-all-start = ((bf16[4,2,2,512,128]{4,3,2,1,0:T(8,128)(2,1)}), bf16[4,2,2,512,128]{4,3,2,1,0:T(8,128)(2,1)S(1)}, u32[]{:S(2)}, u32[]{:S(2)}) async-start(bf16[4,2,2,512,128]{4,3,2,1,0:T(8,128)(2,1)} %pad_maximum_fusion), calls=%async_computation | async-start | bytes 4194304 | tf_op jit(solution)/shard_map/all_to_all | solution.py:127
  8.7 0.0 copy-done.3
  8.7 0.0 copy-done.4
  8.8 0.0 copy-start.2
  8.8 2.9 %collective-permute-start = (bf16[2,2,256,128]{3,2,1,0:T(8,128)(2,1)S(1)}, bf16[2,2,256,128]{3,2,1,0:T(8,128)(2,1)S(1)}, u32[]{:S(2)}, u32[]{:S(2)}) collective-permute-start(bf16[2,2,256,128]{3,2,1,0:T(8,128)(2,1)S(1)} %pad_maximum_fusion.1.own_ref), channel_id=1, source_target_pairs={{0,8},{4,12},{8,16},{12,20},{16,24},{20,28},{1,9},{5,13},{9,17},{1... | collective-permute-start | bytes 786440 | tf_op jit(solution)/shard_map/ppermute | solution.py:19
  11.8 4.1 %collective-permute-start.1 = (bf16[2,2,256,128]{3,2,1,0:T(8,128)(2,1)S(1)}, bf16[2,2,256,128]{3,2,1,0:T(8,128)(2,1)S(1)}, u32[]{:S(2)}, u32[]{:S(2)}) collective-permute-start(bf16[2,2,256,128]{3,2,1,0:T(8,128)(2,1)S(1)} %pad_maximum_fusion.1.own_ref), channel_id=1, source_target_pairs={{0,4},{4,8},{8,12},{12,16},{16,20},{20,24},{24,28},{1,5},{5,9},{9,... | collective-permute-start | bytes 786440 | tf_op jit(solution)/shard_map/ppermute | solution.py:19
  15.9 0.0 copy-done.9
  15.9 0.5 compare_select_fusion.bias_ref
  16.4 9.0 %collective-permute-done.far_ref = bf16[2,2,256,128]{3,2,1,0:T(8,128)(2,1)S(1)} collective-permute-done((bf16[2,2,256,128]{3,2,1,0:T(8,128)(2,1)S(1)}, bf16[2,2,256,128]{3,2,1,0:T(8,128)(2,1)S(1)}, u32[]{:S(2)}, u32[]{:S(2)}) %collective-permute-start) | collective-permute-done | bytes 262176 | tf_op jit(solution)/shard_map/ppermute | solution.py:19
  25.4 0.0 copy-start.5
  25.4 0.9 %collective-permute-done.1.near_ref = bf16[2,2,256,128]{3,2,1,0:T(8,128)(2,1)S(1)} collective-permute-done((bf16[2,2,256,128]{3,2,1,0:T(8,128)(2,1)S(1)}, bf16[2,2,256,128]{3,2,1,0:T(8,128)(2,1)S(1)}, u32[]{:S(2)}, u32[]{:S(2)}) %collective-permute-start.1) | collective-permute-done | bytes 262176 | tf_op jit(solution)/shard_map/ppermute | solution.py:19
  26.4 0.0 copy-start.6
  26.4 6.2 %all-to-all-done.q_ref.do_ref = bf16[4,2,2,512,128]{4,3,2,1,0:T(8,128)(2,1)S(1)} async-done(((bf16[4,2,2,512,128]{4,3,2,1,0:T(8,128)(2,1)}), bf16[4,2,2,512,128]{4,3,2,1,0:T(8,128)(2,1)S(1)}, u32[]{:S(2)}, u32[]{:S(2)}) %all-to-all-start) | async-done | bytes 2097184 | tf_op jit(solution)/shard_map/all_to_all | solution.py:127
  32.6 0.0 copy-done.2
  32.6 0.0 copy-done.5
  32.6 0.0 copy-done.6
  32.6 0.0 copy-start
  32.6 1.3 %copy-done = bf16[4,2,2,512,128]{4,3,2,1,0:T(8,128)(2,1)} copy-done((bf16[4,2,2,512,128]{4,3,2,1,0:T(8,128)(2,1)}, bf16[4,2,2,512,128]{4,3,2,1,0:T(8,128)(2,1)S(1)}, u32[]{:S(2)}) %copy-start) | copy-done | bytes 2097176
  33.9 17.0 %grads.1 = (bf16[4,2,512,128]{3,2,1,0:T(8,128)(2,1)}, bf16[2,2,256,128]{3,2,1,0:T(8,128)(2,1)}, bf16[2,2,256,128]{3,2,1,0:T(8,128)(2,1)}, f32[2,2,256,128]{3,2,1,0:T(8,128)}) custom-call(f32[2]{0:T(128)} %compare_select_fusion.bias_ref, bf16[4,2,2,512,128]{4,3,2,1,0:T(8,128)(2,1)} %copy-done, bf16[4,2,2,512,128]{4,3,2,1,0:T(8,128)(2,1)} %copy-done, ...), custom_call_target="tpu_custom_call" | custom-call | flops 4026531840 | bytes 2097152 | tf_op jit(solution)/shard_map/grads/pallas_call | solution.py:88
  50.9 0.0 copy-start.8
  50.9 0.0 copy-start.7
  50.9 0.0 copy-start.1
  50.9 5.5 %all-to-all-start.1 = ((bf16[4,2,512,128]{3,2,1,0:T(8,128)(2,1)}), bf16[4,2,512,128]{3,2,1,0:T(8,128)(2,1)S(1)}, u32[]{:S(2)}, u32[]{:S(2)}) async-start(bf16[4,2,512,128]{3,2,1,0:T(8,128)(2,1)} %get-tuple-element.7), calls=%async_computation.1 | async-start | bytes 2097152 | tf_op jit(solution)/shard_map/all_to_all | solution.py:132
  56.4 0.0 copy-done.8
  56.4 2.0 %collective-permute-start.3 = (bf16[2,2,256,128]{3,2,1,0:T(8,128)(2,1)S(1)}, bf16[2,2,256,128]{3,2,1,0:T(8,128)(2,1)S(1)}, u32[]{:S(2)}, u32[]{:S(2)}) collective-permute-start(bf16[2,2,256,128]{3,2,1,0:T(8,128)(2,1)S(1)} %copy-done.8), channel_id=1, source_target_pairs={{8,0},{12,4},{16,8},{20,12},{24,16},{28,20},{9,1},{13,5},{17,9},{2... | collective-permute-start | bytes 786440 | tf_op jit(solution)/shard_map/ppermute | solution.py:19
  58.4 0.0 copy-done.7
  58.4 2.0 %collective-permute-start.2 = (bf16[2,2,256,128]{3,2,1,0:T(8,128)(2,1)S(1)}, bf16[2,2,256,128]{3,2,1,0:T(8,128)(2,1)S(1)}, u32[]{:S(2)}, u32[]{:S(2)}) collective-permute-start(bf16[2,2,256,128]{3,2,1,0:T(8,128)(2,1)S(1)} %copy-done.7), channel_id=1, source_target_pairs={{4,0},{8,4},{12,8},{16,12},{20,16},{24,20},{28,24},{5,1},{9,5},{13... | collective-permute-start | bytes 786440 | tf_op jit(solution)/shard_map/ppermute | solution.py:19
  60.4 19.0 %collective-permute-done.3 = bf16[2,2,256,128]{3,2,1,0:T(8,128)(2,1)S(1)} collective-permute-done((bf16[2,2,256,128]{3,2,1,0:T(8,128)(2,1)S(1)}, bf16[2,2,256,128]{3,2,1,0:T(8,128)(2,1)S(1)}, u32[]{:S(2)}, u32[]{:S(2)}) %collective-permute-start.3) | collective-permute-done | bytes 262176 | tf_op jit(solution)/shard_map/ppermute | solution.py:19
  79.4 0.0 collective-permute-done.2
  79.4 0.0 copy-done.1
  79.4 0.1 fusion
  79.6 0.8 copy.13
  80.4 0.8 copy.14
  81.2 0.0 all-to-all-done.1
  81.2 1.3 %copy.12 = bf16[64,4,2,8,128]{4,3,2,1,0:T(8,128)(2,1)} copy(bf16[64,4,2,8,128]{4,3,0,2,1:T(8,128)(2,1)S(1)} %bitcast.28) | data formatting | bytes 2097152 | tf_op jit(solution)/shard_map/transpose | solution.py:133
  (3 shorter events, 0.1 us)
Async XLA Ops:
  4.2 4.5 %copy-start.3 = (bf16[256,2,128]{2,1,0:T(2,128)(2,1)S(1)}, bf16[256,2,128]{2,1,0:T(2,128)(2,1)}, u32[]{:S(2)}) copy-start(bf16[256,2,128]{2,1,0:T(2,128)(2,1)} %param.7) | copy-start | bytes 393220
  4.2 4.5 %copy-start.4 = (bf16[256,2,128]{2,1,0:T(2,128)(2,1)S(1)}, bf16[256,2,128]{2,1,0:T(2,128)(2,1)}, u32[]{:S(2)}) copy-start(bf16[256,2,128]{2,1,0:T(2,128)(2,1)} %param.6) | copy-start | bytes 393220
  4.2 11.7 %copy-start.9 = (s32[2]{0:T(128)S(1)}, s32[2]{0:T(128)}, u32[]{:S(2)}) copy-start(s32[2]{0:T(128)} %constant.19.clone) | copy-start | bytes 28
  4.2 28.3 %all-to-all-start = ((bf16[4,2,2,512,128]{4,3,2,1,0:T(8,128)(2,1)}), bf16[4,2,2,512,128]{4,3,2,1,0:T(8,128)(2,1)S(1)}, u32[]{:S(2)}, u32[]{:S(2)}) async-start(bf16[4,2,2,512,128]{4,3,2,1,0:T(8,128)(2,1)} %pad_maximum_fusion), calls=%async_computation | async-start | bytes 4194304 | tf_op jit(solution)/shard_map/all_to_all | solution.py:127
  8.8 23.7 %copy-start.2 = (bf16[2,2,256,128]{3,2,1,0:T(8,128)(2,1)}, bf16[2,2,256,128]{3,2,1,0:T(8,128)(2,1)S(1)}, u32[]{:S(2)}) copy-start(bf16[2,2,256,128]{3,2,1,0:T(8,128)(2,1)S(1)} %pad_maximum_fusion.1.own_ref) | copy-start | bytes 786436
  8.8 16.6 %collective-permute-start = (bf16[2,2,256,128]{3,2,1,0:T(8,128)(2,1)S(1)}, bf16[2,2,256,128]{3,2,1,0:T(8,128)(2,1)S(1)}, u32[]{:S(2)}, u32[]{:S(2)}) collective-permute-start(bf16[2,2,256,128]{3,2,1,0:T(8,128)(2,1)S(1)} %pad_maximum_fusion.1.own_ref), channel_id=1, source_target_pairs={{0,8},{4,12},{8,16},{12,20},{16,24},{20,28},{1,9},{5,13},{9,17},{1... | collective-permute-start | bytes 786440 | tf_op jit(solution)/shard_map/ppermute | solution.py:19
  11.8 14.6 %collective-permute-start.1 = (bf16[2,2,256,128]{3,2,1,0:T(8,128)(2,1)S(1)}, bf16[2,2,256,128]{3,2,1,0:T(8,128)(2,1)S(1)}, u32[]{:S(2)}, u32[]{:S(2)}) collective-permute-start(bf16[2,2,256,128]{3,2,1,0:T(8,128)(2,1)S(1)} %pad_maximum_fusion.1.own_ref), channel_id=1, source_target_pairs={{0,4},{4,8},{8,12},{12,16},{16,20},{20,24},{24,28},{1,5},{5,9},{9,... | collective-permute-start | bytes 786440 | tf_op jit(solution)/shard_map/ppermute | solution.py:19
  25.4 7.2 %copy-start.5 = (bf16[2,2,256,128]{3,2,1,0:T(8,128)(2,1)}, bf16[2,2,256,128]{3,2,1,0:T(8,128)(2,1)S(1)}, u32[]{:S(2)}) copy-start(bf16[2,2,256,128]{3,2,1,0:T(8,128)(2,1)S(1)} %collective-permute-done.far_ref) | copy-start | bytes 786436
  26.4 6.2 %copy-start.6 = (bf16[2,2,256,128]{3,2,1,0:T(8,128)(2,1)}, bf16[2,2,256,128]{3,2,1,0:T(8,128)(2,1)S(1)}, u32[]{:S(2)}) copy-start(bf16[2,2,256,128]{3,2,1,0:T(8,128)(2,1)S(1)} %collective-permute-done.1.near_ref) | copy-start | bytes 786436
  32.6 1.3 %copy-start = (bf16[4,2,2,512,128]{4,3,2,1,0:T(8,128)(2,1)}, bf16[4,2,2,512,128]{4,3,2,1,0:T(8,128)(2,1)S(1)}, u32[]{:S(2)}) copy-start(bf16[4,2,2,512,128]{4,3,2,1,0:T(8,128)(2,1)S(1)} %all-to-all-done.q_ref.do_ref) | copy-start | bytes 6291460
  50.9 5.5 %copy-start.8 = (bf16[2,2,256,128]{3,2,1,0:T(8,128)(2,1)S(1)}, bf16[2,2,256,128]{3,2,1,0:T(8,128)(2,1)}, u32[]{:S(2)}) copy-start(bf16[2,2,256,128]{3,2,1,0:T(8,128)(2,1)} %get-tuple-element.10) | copy-start | bytes 786436
  50.9 7.5 %copy-start.7 = (bf16[2,2,256,128]{3,2,1,0:T(8,128)(2,1)S(1)}, bf16[2,2,256,128]{3,2,1,0:T(8,128)(2,1)}, u32[]{:S(2)}) copy-start(bf16[2,2,256,128]{3,2,1,0:T(8,128)(2,1)} %get-tuple-element.9) | copy-start | bytes 786436
  50.9 28.5 %copy-start.1 = (f32[2,2,256,128]{3,2,1,0:T(8,128)S(1)}, f32[2,2,256,128]{3,2,1,0:T(8,128)}, u32[]{:S(2)}) copy-start(f32[2,2,256,128]{3,2,1,0:T(8,128)} %get-tuple-element.8) | copy-start | bytes 1572868
  50.9 30.3 %all-to-all-start.1 = ((bf16[4,2,512,128]{3,2,1,0:T(8,128)(2,1)}), bf16[4,2,512,128]{3,2,1,0:T(8,128)(2,1)S(1)}, u32[]{:S(2)}, u32[]{:S(2)}) async-start(bf16[4,2,512,128]{3,2,1,0:T(8,128)(2,1)} %get-tuple-element.7), calls=%async_computation.1 | async-start | bytes 2097152 | tf_op jit(solution)/shard_map/all_to_all | solution.py:132
  56.4 23.0 %collective-permute-start.3 = (bf16[2,2,256,128]{3,2,1,0:T(8,128)(2,1)S(1)}, bf16[2,2,256,128]{3,2,1,0:T(8,128)(2,1)S(1)}, u32[]{:S(2)}, u32[]{:S(2)}) collective-permute-start(bf16[2,2,256,128]{3,2,1,0:T(8,128)(2,1)S(1)} %copy-done.8), channel_id=1, source_target_pairs={{8,0},{12,4},{16,8},{20,12},{24,16},{28,20},{9,1},{13,5},{17,9},{2... | collective-permute-start | bytes 786440 | tf_op jit(solution)/shard_map/ppermute | solution.py:19
  58.4 21.1 %collective-permute-start.2 = (bf16[2,2,256,128]{3,2,1,0:T(8,128)(2,1)S(1)}, bf16[2,2,256,128]{3,2,1,0:T(8,128)(2,1)S(1)}, u32[]{:S(2)}, u32[]{:S(2)}) collective-permute-start(bf16[2,2,256,128]{3,2,1,0:T(8,128)(2,1)S(1)} %copy-done.7), channel_id=1, source_target_pairs={{4,0},{8,4},{12,8},{16,12},{20,16},{24,20},{28,24},{5,1},{9,5},{13... | collective-permute-start | bytes 786440 | tf_op jit(solution)/shard_map/ppermute | solution.py:19

commit v2 on v1

v2 whole, which is shorter than its diff:
```python
import functools
import math

import jax
import jax.numpy as jnp
from jax import lax
from jax.experimental import pallas as pl
from jax.experimental.pallas import tpu as pltpu
from jax.sharding import PartitionSpec as P


NT = (((1,), (1,)), ((), ()))
SEQ = ("inner", "outer")
NEVER = 1e30
VMEM = pl.BlockSpec(memory_space=pltpu.VMEM)
HBM = pl.BlockSpec(memory_space=pltpu.HBM)


def shifted(value, by):
    peers = lax.axis_size(SEQ)
    pairs = [(i, i + by) for i in range(peers) if 0 <= i + by < peers]
    return lax.ppermute(value, SEQ, pairs)


def swapped(value, distance):
    peers = lax.axis_size("head")
    return lax.ppermute(value, "head", [(i, i ^ distance) for i in range(peers)])


def pack_kernel(parts, q_ref, do_ref, *refs):
    outs, sem = refs[:-1], refs[-1]
    me = lax.axis_index("head")
    kv_heads = q_ref.shape[1] // lax.axis_size("head")
    copies = []
    for out, part in zip(outs, parts):
        for n, (kv, distance) in enumerate(part):
            place = (me ^ distance) * kv_heads + kv
            for which, source in enumerate((q_ref, do_ref)):
                copies.append(
                    pltpu.make_async_copy(source.at[:, place], out.at[n, which], sem.at[len(copies)])
                )
    for copy in copies:
        copy.start()
    for copy in copies:
        copy.wait()


def pack(queries, grad_out, parts):
    part_rows, _, group, width = queries.shape
    return pl.pallas_call(
        functools.partial(pack_kernel, parts),
        in_specs=[HBM, HBM],
        out_specs=[VMEM] * len(parts),
        out_shape=[
            jax.ShapeDtypeStruct((len(part), 2, part_rows, group, width), queries.dtype)
            for part in parts
        ],
        scratch_shapes=[pltpu.SemaphoreType.DMA((2 * sum(len(part) for part in parts),))],
        compiler_params=pltpu.CompilerParams(vmem_limit_bytes=16 * 2**20),
        name="pack",
    )(queries, grad_out)


def unpack_kernel(parts, *refs):
    values, out_ref, sem = refs[:-2], refs[-2], refs[-1]
    me = lax.axis_index("head")
    kv_heads = out_ref.shape[1] // lax.axis_size("head")
    copies = []
    for value, part in zip(values, parts):
        for n, (kv, distance) in enumerate(part):
            place = (me ^ distance) * kv_heads + kv
            copies.append(
                pltpu.make_async_copy(value.at[n], out_ref.at[:, place], sem.at[len(copies)])
            )
    for copy in copies:
        copy.start()
    for copy in copies:
        copy.wait()


def unpack(values, parts, places):
    _, part_rows, group, width = values[0].shape
    return pl.pallas_call(
        functools.partial(unpack_kernel, parts),
        in_specs=[VMEM] * len(values),
        out_specs=HBM,
        out_shape=jax.ShapeDtypeStruct((part_rows, places, group, width), values[0].dtype),
        scratch_shapes=[pltpu.SemaphoreType.DMA((sum(len(part) for part in parts),))],
        compiler_params=pltpu.CompilerParams(vmem_limit_bytes=16 * 2**20),
        name="unpack",
    )(*values)


def grads_kernel(where, *refs):
    peers = len(where)
    pair_refs, (far_ref, near_ref, own_ref) = refs[:peers], refs[peers : peers + 3]
    dq_refs, (dfar_ref, dnear_ref, down_ref) = (
        refs[peers + 3 : 2 * peers + 3],
        refs[2 * peers + 3 : 2 * peers + 6],
    )
    pairs, dqs, acc, kt = refs[2 * peers + 6 :]
    windows = (far_ref, near_ref, own_ref)
    _, part_rows, group, width = pair_refs[0].shape[1:]
    rows = part_rows * group
    scale = width ** (-0.5)
    to_exp2 = scale * math.log2(math.e)
    me = lax.axis_index("head")
    block = lax.axis_index(SEQ)
    bias = (
        jnp.where(block < 2, NEVER, 0.0).astype(jnp.float32),
        jnp.where(block < 1, NEVER, 0.0).astype(jnp.float32),
        0.0,
    )
    for d in range(peers):
        pairs[d] = pair_refs[d][where[d]].reshape(2, rows, width)
    for j, window in enumerate(windows):
        kt[j] = window[0].T
    acc[...] = jnp.zeros_like(acc)

    def step(d, carry):
        q = pairs[d, 0]
        do = pairs[d, 1]
        first = (me ^ d) * rows
        scores, tops = [], []
        for j, window in enumerate(windows):
            s = lax.dot_general(window[0], q, NT, preferred_element_type=jnp.float32)
            if j == 2:
                token = (lax.broadcasted_iota(jnp.int32, s.shape, 1) + first) // group
                key = lax.broadcasted_iota(jnp.int32, s.shape, 0)
                s = jnp.where(key <= token, s, -jnp.inf)
            scores.append(s)
            tops.append(jnp.max(s, axis=0, keepdims=True) - bias[j])
        top = jnp.maximum(jnp.maximum(tops[0], tops[1]), tops[2]) * to_exp2
        weights, dprobs, total, dtotal = [], [], 0.0, 0.0
        for j, window in enumerate(windows):
            e = jnp.exp2(scores[j] * to_exp2 - (top + bias[j]))
            dp = lax.dot_general(window[1], do, NT, preferred_element_type=jnp.float32)
            total = total + jnp.sum(e, axis=0, keepdims=True)
            dtotal = dtotal + jnp.sum(e * dp, axis=0, keepdims=True)
            weights.append(e)
            dprobs.append(dp)
        inverse = 1.0 / total
        delta = dtotal * inverse
        dqt = 0.0
        for j in range(3):
            p = weights[j] * inverse
            ds = (p * (dprobs[j] - delta)).astype(jnp.bfloat16)
            acc[j, 1] += jnp.dot(p.astype(jnp.bfloat16), do, preferred_element_type=jnp.float32)
            acc[j, 0] += jnp.dot(ds, q, preferred_element_type=jnp.float32)
            dqt = dqt + jnp.dot(kt[j], ds, preferred_element_type=jnp.float32)
        dqs[d] = (dqt * scale).T.astype(dqs.dtype)
        return carry

    lax.fori_loop(0, peers, step, 0)
    for d in range(peers):
        dq_refs[d][0] = dqs[d].reshape(part_rows, group, width)
    for j, out in enumerate((dfar_ref, dnear_ref, down_ref)):
        out[0] = (acc[j, 0] * scale).astype(out.dtype)
        out[1] = acc[j, 1].astype(out.dtype)


def group_grads(pairs, where, far, near, own):
    peers = len(pairs)
    _, _, part_rows, group, width = pairs[0].shape
    tok_rows = own.shape[1]
    rows = part_rows * group
    window = (2, tok_rows, width)
    cells = peers * rows * 3 * tok_rows
    outs = pl.pallas_call(
        functools.partial(grads_kernel, where),
        in_specs=[VMEM] * (peers + 3),
        out_specs=[VMEM] * (peers + 3),
        out_shape=[jax.ShapeDtypeStruct((1, part_rows, group, width), jnp.bfloat16)] * peers
        + [
            jax.ShapeDtypeStruct(window, jnp.bfloat16),
            jax.ShapeDtypeStruct(window, jnp.bfloat16),
            jax.ShapeDtypeStruct(window, jnp.float32),
        ],
        scratch_shapes=[
            pltpu.VMEM((peers, 2, rows, width), jnp.bfloat16),
            pltpu.VMEM((peers, rows, width), jnp.bfloat16),
            pltpu.VMEM((3, 2, tok_rows, width), jnp.float32),
            pltpu.VMEM((3, width, tok_rows), jnp.bfloat16),
        ],
        compiler_params=pltpu.CompilerParams(vmem_limit_bytes=32 * 2**20),
        cost_estimate=pl.CostEstimate(
            flops=10 * cells * width, bytes_accessed=6 * peers * rows * width, transcendentals=cells
        ),
        name="grads",
    )(*pairs, far, near, own)
    return outs[:peers], outs[peers:]


def shards(queries, key_vector_rows, value_vector_rows, grad_out):
    part_rows, heads, width = queries.shape
    kv_heads = key_vector_rows.shape[1]
    peers = lax.axis_size("head")
    group = heads // (peers * kv_heads)
    places = peers * kv_heads
    queries = queries.reshape(part_rows, places, group, width)
    grad_out = grad_out.reshape(part_rows, places, group, width)
    far_cores = list(range(2, peers))
    all_kv = list(range(kv_heads))

    first = pack(queries, grad_out, [[(0, d)] for d in far_cores])
    rest = pack(
        queries,
        grad_out,
        [[(kv, 0) for kv in all_kv], [(kv, 1) for kv in all_kv]]
        + [[(kv, d)] for kv in all_kv[1:] for d in far_cores],
    )
    sent = [first] + [rest[2 + n * len(far_cores) :][: len(far_cores)] for n in range(kv_heads - 1)]
    crossed, windows = [], []
    for kv in all_kv:
        values = []
        for value, d in zip(sent[kv], far_cores):
            values.append(swapped(value, d))
        crossed.append(values)
        own = jnp.stack([key_vector_rows[:, kv], value_vector_rows[:, kv]], axis=0)
        far = shifted(own, 2)
        near = shifted(own, 1)
        windows.append((far, near, own))
    here = rest[0]
    partner = swapped(rest[1], 1)
    dq_here, dq_partner, dq_crossed, dkeys, dvalues = [], [], [], [], []
    for kv in all_kv:
        dq, (dfar, dnear, down) = group_grads(
            [here, partner] + crossed[kv], [kv, kv] + [0] * len(far_cores), *windows[kv]
        )
        dfar = shifted(dfar, -2)
        dnear = shifted(dnear, -1)
        dq_here.append(dq[0])
        dq_partner.append(dq[1])
        values = []
        for value, d in zip(dq[2:], far_cores):
            values.append(swapped(value, d))
        dq_crossed.append(values)
        total = down + dfar.astype(jnp.float32) + dnear.astype(jnp.float32)
        total = total.astype(jnp.bfloat16)
        dkeys.append(total[0])
        dvalues.append(total[1])
    dq_partner = swapped(jnp.concatenate(dq_partner, axis=0), 1)
    values = dq_here + [dq_partner] + sum(dq_crossed, [])
    parts = [[(kv, 0)] for kv in all_kv] + [[(kv, 1) for kv in all_kv]]
    parts += [[(kv, d)] for kv in all_kv for d in far_cores]
    query_grads = unpack(values, parts, places)
    return (
        query_grads.reshape(part_rows, heads, width),
        jnp.stack(dkeys, axis=1),
        jnp.stack(dvalues, axis=1),
    )


def solution(mesh):
    return jax.shard_map(
        shards,
        mesh=mesh,
        in_specs=(
            P(("inner", "outer", "head"), None, None),
            P(("inner", "outer"), "head", None),
            P(("inner", "outer"), "head", None),
            P(("inner", "outer", "head"), None, None),
        ),
        out_specs=(
            P(("inner", "outer", "head"), None, None),
            P(("inner", "outer"), "head", None),
            P(("inner", "outer"), "head", None),
        ),
        check_vma=False,
    )
```

time: 82.8 us -> 73 us (0.88)
  the two profiles are of different devices: /device:TPU:27 before, /device:TPU:25 now
where the time goes in v2:
time: 73 us; the launch traced here: 72.6 us
  starting transfers between devices  33.3 us (46%)
  waiting for transfers between devices  17.4 us (24%)
  Pallas kernels  16.3 us (22%)
  local copies, waits for them, and re-layouts  4.47 us (6%)
  between operations  0.89 us (1%)
    ppermute x8, starting transfers between devices, shifted(): return lax.ppermute(value, SEQ, pairs)  21 us
    pallas_call x2, Pallas kernels, group_grads(): pl.pallas_call(functools.partial(grads_kernel, where), in_specs=[VMEM] *...  14.6 us
    ppermute x10, starting transfers between devices, swapped(): lax.ppermute(value, 'head', [(i, i ^ distance) for i in range(peers)])  12.3 us
    ppermute x10, waiting for transfers between devices, swapped(): lax.ppermute(value, 'head', [(i, i ^ distance) for i in range(peers)])  8.86 us
    ppermute x8, waiting for transfers between devices, shifted(): return lax.ppermute(value, SEQ, pairs)  8.57 us
    unnamed x10, local copies, waits for them, and re-layouts  4.03 us
  transfers between devices with their start and end apart: 18, of which 4 were waited for; matrix products, arithmetic and copies ran while one was open for 3% of the time, Pallas kernels for 20%

profile of v2, /device:TPU:25, one launch (start us, length us, event | category | flops | bytes accessed | tf_op | source)
XLA Modules:
  0.0 72.6 jit_solution(11415151252462057421)
XLA Ops:
  0.6 0.0 copy-start
  0.6 1.2 %copy-done = bf16[64,64,128]{2,1,0:T(8,128)(2,1)S(1)} copy-done((bf16[64,64,128]{2,1,0:T(8,128)(2,1)S(1)}, bf16[64,64,128]{2,1,0:T(8,128)(2,1)}, u32[]{:S(2)}) %copy-start) | copy-done | bytes 1048600
  1.9 0.0 copy-start.1
  1.9 1.2 %copy-done.1 = bf16[64,64,128]{2,1,0:T(8,128)(2,1)S(1)} copy-done((bf16[64,64,128]{2,1,0:T(8,128)(2,1)S(1)}, bf16[64,64,128]{2,1,0:T(8,128)(2,1)}, u32[]{:S(2)}) %copy-start.1) | copy-done | bytes 1048600
  3.1 0.0 copy-start.2
  3.1 0.5 pack.2
  3.6 0.0 copy-start.3
  3.6 0.7 %collective-permute-start = (bf16[2,2,64,8,128]{4,3,2,1,0:T(8,128)(2,1)S(1)}, bf16[2,2,64,8,128]{4,3,2,1,0:T(8,128)(2,1)S(1)}, u32[]{:S(2)}, u32[]{:S(2)}) collective-permute-start(bf16[2,2,64,8,128]{4,3,2,1,0:T(8,128)(2,1)S(1)} %get-tuple-element.24), channel_id=1, source_target_pairs={{0,1},{1,0},{2,3},{3,2},{4,5},{5,4},{6,7},{7,6},{8,9},{9,8},{10,11... | collective-permute-start | bytes 1572872 | tf_op jit(solution)/shard_map/ppermute | solution.py:27
  4.4 0.0 copy-done.2
  4.4 0.2 fusion
  4.6 0.0 copy-done.3
  4.6 0.2 fusion.1
  4.8 2.9 %collective-permute-start.3 = (bf16[2,256,128]{2,1,0:T(8,128)(2,1)S(1)}, bf16[2,256,128]{2,1,0:T(8,128)(2,1)S(1)}, u32[]{:S(2)}, u32[]{:S(2)}) collective-permute-start(bf16[2,256,128]{2,1,0:T(8,128)(2,1)S(1)} %pad_maximum_fusion.1.refs_6_), channel_id=1, source_target_pairs={{0,8},{4,12},{8,16},{12,20},{16,24},{20,28},{1,9},{5,13},{9,17},{1... | collective-permute-start | bytes 393224 | tf_op jit(solution)/shard_map/ppermute | solution.py:22
  7.8 4.1 %collective-permute-start.4 = (bf16[2,256,128]{2,1,0:T(8,128)(2,1)S(1)}, bf16[2,256,128]{2,1,0:T(8,128)(2,1)S(1)}, u32[]{:S(2)}, u32[]{:S(2)}) collective-permute-start(bf16[2,256,128]{2,1,0:T(8,128)(2,1)S(1)} %pad_maximum_fusion.1.refs_6_), channel_id=1, source_target_pairs={{0,4},{4,8},{8,12},{12,16},{16,20},{20,24},{24,28},{1,5},{5,9},{9,... | collective-permute-start | bytes 393224 | tf_op jit(solution)/shard_map/ppermute | solution.py:22
  11.9 0.2 pack.3
  12.1 1.3 %collective-permute-start.1 = (bf16[1,2,64,8,128]{4,3,2,1,0:T(8,128)(2,1)S(1)}, bf16[1,2,64,8,128]{4,3,2,1,0:T(8,128)(2,1)S(1)}, u32[]{:S(2)}, u32[]{:S(2)}) collective-permute-start(bf16[1,2,64,8,128]{4,3,2,1,0:T(8,128)(2,1)S(1)} %get-tuple-element.25), channel_id=1, source_target_pairs={{0,2},{1,3},{2,0},{3,1},{4,6},{5,7},{6,4},{7,5},{8,10},{9,11},{10,... | collective-permute-start | bytes 786440 | tf_op jit(solution)/shard_map/ppermute | solution.py:27
  13.3 1.6 %collective-permute-start.2 = (bf16[1,2,64,8,128]{4,3,2,1,0:T(8,128)(2,1)S(1)}, bf16[1,2,64,8,128]{4,3,2,1,0:T(8,128)(2,1)S(1)}, u32[]{:S(2)}, u32[]{:S(2)}) collective-permute-start(bf16[1,2,64,8,128]{4,3,2,1,0:T(8,128)(2,1)S(1)} %get-tuple-element.26), channel_id=1, source_target_pairs={{0,3},{1,2},{2,1},{3,0},{4,7},{5,6},{6,5},{7,4},{8,11},{9,10},{10,... | collective-permute-start | bytes 786440 | tf_op jit(solution)/shard_map/ppermute | solution.py:27
  15.0 0.8 %collective-permute-done.3.refs_4_ = bf16[2,256,128]{2,1,0:T(8,128)(2,1)S(1)} collective-permute-done((bf16[2,256,128]{2,1,0:T(8,128)(2,1)S(1)}, bf16[2,256,128]{2,1,0:T(8,128)(2,1)S(1)}, u32[]{:S(2)}, u32[]{:S(2)}) %collective-permute-start.3) | collective-permute-done | bytes 131104 | tf_op jit(solution)/shard_map/ppermute | solution.py:22
  15.8 1.2 %collective-permute-start.5 = (bf16[1,2,64,8,128]{4,3,2,1,0:T(8,128)(2,1)S(1)}, bf16[1,2,64,8,128]{4,3,2,1,0:T(8,128)(2,1)S(1)}, u32[]{:S(2)}, u32[]{:S(2)}) collective-permute-start(bf16[1,2,64,8,128]{4,3,2,1,0:T(8,128)(2,1)S(1)} %get-tuple-element.28), channel_id=1, source_target_pairs={{0,2},{1,3},{2,0},{3,1},{4,6},{5,7},{6,4},{7,5},{8,10},{9,11},{10,... | collective-permute-start | bytes 786440 | tf_op jit(solution)/shard_map/ppermute | solution.py:27
  17.0 0.0 collective-permute-done.4.refs_5_
  17.0 2.4 %collective-permute-start.6 = (bf16[1,2,64,8,128]{4,3,2,1,0:T(8,128)(2,1)S(1)}, bf16[1,2,64,8,128]{4,3,2,1,0:T(8,128)(2,1)S(1)}, u32[]{:S(2)}, u32[]{:S(2)}) collective-permute-start(bf16[1,2,64,8,128]{4,3,2,1,0:T(8,128)(2,1)S(1)} %get-tuple-element.29), channel_id=1, source_target_pairs={{0,3},{1,2},{2,1},{3,0},{4,7},{5,6},{6,5},{7,4},{8,11},{9,10},{10,... | collective-permute-start | bytes 786440 | tf_op jit(solution)/shard_map/ppermute | solution.py:27
  19.4 0.0 collective-permute-done.1.refs_2_
  19.4 2.9 %collective-permute-start.7 = (bf16[2,256,128]{2,1,0:T(8,128)(2,1)S(1)}, bf16[2,256,128]{2,1,0:T(8,128)(2,1)S(1)}, u32[]{:S(2)}, u32[]{:S(2)}) collective-permute-start(bf16[2,256,128]{2,1,0:T(8,128)(2,1)S(1)} %pad_maximum_fusion.2.refs_6_), channel_id=1, source_target_pairs={{0,8},{4,12},{8,16},{12,20},{16,24},{20,28},{1,9},{5,13},{9,17},{1... | collective-permute-start | bytes 393224 | tf_op jit(solution)/shard_map/ppermute | solution.py:22
  22.4 5.1 %collective-permute-done.2.refs_3_ = bf16[1,2,64,8,128]{4,3,2,1,0:T(8,128)(2,1)S(1)} collective-permute-done((bf16[1,2,64,8,128]{4,3,2,1,0:T(8,128)(2,1)S(1)}, bf16[1,2,64,8,128]{4,3,2,1,0:T(8,128)(2,1)S(1)}, u32[]{:S(2)}, u32[]{:S(2)}) %collective-permute-start.2) | collective-permute-done | bytes 262176 | tf_op jit(solution)/shard_map/ppermute | solution.py:27
  27.4 3.2 %collective-permute-start.8 = (bf16[2,256,128]{2,1,0:T(8,128)(2,1)S(1)}, bf16[2,256,128]{2,1,0:T(8,128)(2,1)S(1)}, u32[]{:S(2)}, u32[]{:S(2)}) collective-permute-start(bf16[2,256,128]{2,1,0:T(8,128)(2,1)S(1)} %pad_maximum_fusion.2.refs_6_), channel_id=1, source_target_pairs={{0,4},{4,8},{8,12},{12,16},{16,20},{20,24},{24,28},{1,5},{5,9},{9,... | collective-permute-start | bytes 393224 | tf_op jit(solution)/shard_map/ppermute | solution.py:22
  30.6 0.0 collective-permute-done.refs_1_
  30.7 7.3 %grads.2 = (bf16[1,64,8,128]{3,2,1,0:T(8,128)(2,1)S(1)}, bf16[1,64,8,128]{3,2,1,0:T(8,128)(2,1)S(1)}, bf16[1,64,8,128]{3,2,1,0:T(8,128)(2,1)S(1)}, bf16[1,64,8,1...) custom-call(bf16[2,2,64,8,128]{4,3,2,1,0:T(8,128)(2,1)S(1)} %get-tup, ...), custom_call_target="tpu_custom_call" | custom-call | flops 2013265920 | bytes 1572864 | tf_op jit(solution)/shard_map/grads/pallas_call | solution.py:169
  37.9 1.9 %collective-permute-start.14 = (bf16[2,256,128]{2,1,0:T(8,128)(2,1)S(1)}, bf16[2,256,128]{2,1,0:T(8,128)(2,1)S(1)}, u32[]{:S(2)}, u32[]{:S(2)}) collective-permute-start(bf16[2,256,128]{2,1,0:T(8,128)(2,1)S(1)} %get-tuple-element.38), channel_id=1, source_target_pairs={{8,0},{12,4},{16,8},{20,12},{24,16},{28,20},{9,1},{13,5},{17,9},{2... | collective-permute-start | bytes 393224 | tf_op jit(solution)/shard_map/ppermute | solution.py:22
  39.9 0.0 collective-permute-done.7.refs_4_
  39.9 2.1 %collective-permute-start.15 = (bf16[2,256,128]{2,1,0:T(8,128)(2,1)S(1)}, bf16[2,256,128]{2,1,0:T(8,128)(2,1)S(1)}, u32[]{:S(2)}, u32[]{:S(2)}) collective-permute-start(bf16[2,256,128]{2,1,0:T(8,128)(2,1)S(1)} %get-tuple-element.39), channel_id=1, source_target_pairs={{4,0},{8,4},{12,8},{16,12},{20,16},{24,20},{28,24},{5,1},{9,5},{13... | collective-permute-start | bytes 393224 | tf_op jit(solution)/shard_map/ppermute | solution.py:22
  42.0 0.0 collective-permute-done.8.refs_5_
  42.0 0.0 collective-permute-done.5.refs_2_
  42.0 0.0 collective-permute-done.6.refs_3_
  42.0 7.3 %grads.3 = (bf16[1,64,8,128]{3,2,1,0:T(8,128)(2,1)S(1)}, bf16[1,64,8,128]{3,2,1,0:T(8,128)(2,1)S(1)}, bf16[1,64,8,128]{3,2,1,0:T(8,128)(2,1)S(1)}, bf16[1,64,8,1...) custom-call(bf16[2,2,64,8,128]{4,3,2,1,0:T(8,128)(2,1)S(1)} %get-tup, ...), custom_call_target="tpu_custom_call" | custom-call | flops 2013265920 | bytes 1572864 | tf_op jit(solution)/shard_map/grads/pallas_call | solution.py:169
  49.3 1.9 %collective-permute-start.16 = (bf16[2,256,128]{2,1,0:T(8,128)(2,1)S(1)}, bf16[2,256,128]{2,1,0:T(8,128)(2,1)S(1)}, u32[]{:S(2)}, u32[]{:S(2)}) collective-permute-start(bf16[2,256,128]{2,1,0:T(8,128)(2,1)S(1)} %get-tuple-element.41), channel_id=1, source_target_pairs={{8,0},{12,4},{16,8},{20,12},{24,16},{28,20},{9,1},{13,5},{17,9},{2... | collective-permute-start | bytes 393224 | tf_op jit(solution)/shard_map/ppermute | solution.py:22
  51.2 1.9 %collective-permute-start.17 = (bf16[2,256,128]{2,1,0:T(8,128)(2,1)S(1)}, bf16[2,256,128]{2,1,0:T(8,128)(2,1)S(1)}, u32[]{:S(2)}, u32[]{:S(2)}) collective-permute-start(bf16[2,256,128]{2,1,0:T(8,128)(2,1)S(1)} %get-tuple-element.42), channel_id=1, source_target_pairs={{4,0},{8,4},{12,8},{16,12},{20,16},{24,20},{28,24},{5,1},{9,5},{13... | collective-permute-start | bytes 393224 | tf_op jit(solution)/shard_map/ppermute | solution.py:22
  53.2 0.5 collective-permute-start.9
  53.7 0.0 collective-permute-done.14
  53.7 1.2 %collective-permute-start.12 = (bf16[1,64,8,128]{3,2,1,0:T(8,128)(2,1)S(1)}, bf16[1,64,8,128]{3,2,1,0:T(8,128)(2,1)S(1)}, u32[]{:S(2)}, u32[]{:S(2)}) collective-permute-start(bf16[1,64,8,128]{3,2,1,0:T(8,128)(2,1)S(1)} %get-tuple-element.35), channel_id=1, source_target_pairs={{0,2},{1,3},{2,0},{3,1},{4,6},{5,7},{6,4},{7,5},{8,10},{9,11},{10,... | collective-permute-start | bytes 393224 | tf_op jit(solution)/shard_map/ppermute | solution.py:27
  54.9 0.0 collective-permute-done.15
  54.9 0.5 collective-permute-start.13
  55.5 7.7 %collective-permute-done.16 = bf16[2,256,128]{2,1,0:T(8,128)(2,1)S(1)} collective-permute-done((bf16[2,256,128]{2,1,0:T(8,128)(2,1)S(1)}, bf16[2,256,128]{2,1,0:T(8,128)(2,1)S(1)}, u32[]{:S(2)}, u32[]{:S(2)}) %collective-permute-start.16) | collective-permute-done | bytes 131104 | tf_op jit(solution)/shard_map/ppermute | solution.py:22
  63.3 1.5 %collective-permute-start.10 = (bf16[1,64,8,128]{3,2,1,0:T(8,128)(2,1)S(1)}, bf16[1,64,8,128]{3,2,1,0:T(8,128)(2,1)S(1)}, u32[]{:S(2)}, u32[]{:S(2)}) collective-permute-start(bf16[1,64,8,128]{3,2,1,0:T(8,128)(2,1)S(1)} %get-tuple-element.33), channel_id=1, source_target_pairs={{0,2},{1,3},{2,0},{3,1},{4,6},{5,7},{6,4},{7,5},{8,10},{9,11},{10,... | collective-permute-start | bytes 393224 | tf_op jit(solution)/shard_map/ppermute | solution.py:27
  64.7 0.0 collective-permute-done.17
  64.7 1.4 %collective-permute-start.11 = (bf16[1,64,8,128]{3,2,1,0:T(8,128)(2,1)S(1)}, bf16[1,64,8,128]{3,2,1,0:T(8,128)(2,1)S(1)}, u32[]{:S(2)}, u32[]{:S(2)}) collective-permute-start(bf16[1,64,8,128]{3,2,1,0:T(8,128)(2,1)S(1)} %get-tuple-element.34), channel_id=1, source_target_pairs={{0,3},{1,2},{2,1},{3,0},{4,7},{5,6},{6,5},{7,4},{8,11},{9,10},{10,... | collective-permute-start | bytes 393224 | tf_op jit(solution)/shard_map/ppermute | solution.py:27
  66.2 0.8 %copy.12 = bf16[256,2,128]{2,1,0:T(2,128)(2,1)} copy(bf16[256,2,128]{2,0,1:T(8,128)(2,1)S(1)} %pad_maximum_fusion.4) | data formatting | bytes 262144
  67.1 0.8 %copy.11 = bf16[256,2,128]{2,1,0:T(2,128)(2,1)} copy(bf16[256,2,128]{2,0,1:T(8,128)(2,1)S(1)} %pad_maximum_fusion.3) | data formatting | bytes 262144
  67.8 0.0 collective-permute-done.12.refs_5_
  67.8 0.0 collective-permute-done.13.refs_6_
  67.8 0.0 collective-permute-done.10.refs_3_
  67.9 3.7 %collective-permute-done.11.refs_4_ = bf16[1,64,8,128]{3,2,1,0:T(8,128)(2,1)S(1)} collective-permute-done((bf16[1,64,8,128]{3,2,1,0:T(8,128)(2,1)S(1)}, bf16[1,64,8,128]{3,2,1,0:T(8,128)(2,1)S(1)}, u32[]{:S(2)}, u32[]{:S(2)}) %collective-permute-start.11) | collective-permute-done | bytes 131104 | tf_op jit(solution)/shard_map/ppermute | solution.py:27
  71.6 0.0 collective-permute-done.9.refs_2_
  71.6 1.0 %unpack.1 = bf16[64,8,8,128]{3,2,1,0:T(8,128)(2,1)} custom-call(bf16[1,64,8,128]{3,2,1,0:T(8,128)(2,1)S(1)} %get-tuple-element.27.refs_0_, bf16[1,64,8,128]{3,2,1,0:T(8,128)(2,1)S(1)} %get-tuple-element.30.refs_1_, bf16[2,64,8,128]{3,2,1,0:T(8,128)(2,1)S(1)} %collective-permute-done.9.refs_2_, bf16[1,64,8,128]{3,2,1,0:T(8,128)(2,1)S(1)} %collective-permute-done.10.refs_3_, ...), custom_call_target="tpu_custom_call" | custom-call | tf_op jit(solution)/shard_map/unpack/pallas_call | solution.py:83
  (11 shorter events, 0.2 us)
Async XLA Ops:
  0.6 1.2 %copy-start = (bf16[64,64,128]{2,1,0:T(8,128)(2,1)S(1)}, bf16[64,64,128]{2,1,0:T(8,128)(2,1)}, u32[]{:S(2)}) copy-start(bf16[64,64,128]{2,1,0:T(8,128)(2,1)} %param.4) | copy-start | bytes 3145732
  1.9 1.2 %copy-start.1 = (bf16[64,64,128]{2,1,0:T(8,128)(2,1)S(1)}, bf16[64,64,128]{2,1,0:T(8,128)(2,1)}, u32[]{:S(2)}) copy-start(bf16[64,64,128]{2,1,0:T(8,128)(2,1)} %param.7) | copy-start | bytes 3145732
  3.1 1.3 %copy-start.2 = (bf16[256,2,128]{2,1,0:T(2,128)(2,1)S(1)}, bf16[256,2,128]{2,1,0:T(2,128)(2,1)}, u32[]{:S(2)}) copy-start(bf16[256,2,128]{2,1,0:T(2,128)(2,1)} %param.5) | copy-start | bytes 393220
  3.6 0.9 %copy-start.3 = (bf16[256,2,128]{2,1,0:T(2,128)(2,1)S(1)}, bf16[256,2,128]{2,1,0:T(2,128)(2,1)}, u32[]{:S(2)}) copy-start(bf16[256,2,128]{2,1,0:T(2,128)(2,1)} %param.6) | copy-start | bytes 393220
  3.6 27.0 %collective-permute-start = (bf16[2,2,64,8,128]{4,3,2,1,0:T(8,128)(2,1)S(1)}, bf16[2,2,64,8,128]{4,3,2,1,0:T(8,128)(2,1)S(1)}, u32[]{:S(2)}, u32[]{:S(2)}) collective-permute-start(bf16[2,2,64,8,128]{4,3,2,1,0:T(8,128)(2,1)S(1)} %get-tuple-element.24), channel_id=1, source_target_pairs={{0,1},{1,0},{2,3},{3,2},{4,5},{5,4},{6,7},{7,6},{8,9},{9,8},{10,11... | collective-permute-start | bytes 1572872 | tf_op jit(solution)/shard_map/ppermute | solution.py:27
  4.8 11.0 %collective-permute-start.3 = (bf16[2,256,128]{2,1,0:T(8,128)(2,1)S(1)}, bf16[2,256,128]{2,1,0:T(8,128)(2,1)S(1)}, u32[]{:S(2)}, u32[]{:S(2)}) collective-permute-start(bf16[2,256,128]{2,1,0:T(8,128)(2,1)S(1)} %pad_maximum_fusion.1.refs_6_), channel_id=1, source_target_pairs={{0,8},{4,12},{8,16},{12,20},{16,24},{20,28},{1,9},{5,13},{9,17},{1... | collective-permute-start | bytes 393224 | tf_op jit(solution)/shard_map/ppermute | solution.py:22
  7.8 9.3 %collective-permute-start.4 = (bf16[2,256,128]{2,1,0:T(8,128)(2,1)S(1)}, bf16[2,256,128]{2,1,0:T(8,128)(2,1)S(1)}, u32[]{:S(2)}, u32[]{:S(2)}) collective-permute-start(bf16[2,256,128]{2,1,0:T(8,128)(2,1)S(1)} %pad_maximum_fusion.1.refs_6_), channel_id=1, source_target_pairs={{0,4},{4,8},{8,12},{12,16},{16,20},{20,24},{24,28},{1,5},{5,9},{9,... | collective-permute-start | bytes 393224 | tf_op jit(solution)/shard_map/ppermute | solution.py:22
  12.1 7.3 %collective-permute-start.1 = (bf16[1,2,64,8,128]{4,3,2,1,0:T(8,128)(2,1)S(1)}, bf16[1,2,64,8,128]{4,3,2,1,0:T(8,128)(2,1)S(1)}, u32[]{:S(2)}, u32[]{:S(2)}) collective-permute-start(bf16[1,2,64,8,128]{4,3,2,1,0:T(8,128)(2,1)S(1)} %get-tuple-element.25), channel_id=1, source_target_pairs={{0,2},{1,3},{2,0},{3,1},{4,6},{5,7},{6,4},{7,5},{8,10},{9,11},{10,... | collective-permute-start | bytes 786440 | tf_op jit(solution)/shard_map/ppermute | solution.py:27
  13.3 14.1 %collective-permute-start.2 = (bf16[1,2,64,8,128]{4,3,2,1,0:T(8,128)(2,1)S(1)}, bf16[1,2,64,8,128]{4,3,2,1,0:T(8,128)(2,1)S(1)}, u32[]{:S(2)}, u32[]{:S(2)}) collective-permute-start(bf16[1,2,64,8,128]{4,3,2,1,0:T(8,128)(2,1)S(1)} %get-tuple-element.26), channel_id=1, source_target_pairs={{0,3},{1,2},{2,1},{3,0},{4,7},{5,6},{6,5},{7,4},{8,11},{9,10},{10,... | collective-permute-start | bytes 786440 | tf_op jit(solution)/shard_map/ppermute | solution.py:27
  15.8 26.2 %collective-permute-start.5 = (bf16[1,2,64,8,128]{4,3,2,1,0:T(8,128)(2,1)S(1)}, bf16[1,2,64,8,128]{4,3,2,1,0:T(8,128)(2,1)S(1)}, u32[]{:S(2)}, u32[]{:S(2)}) collective-permute-start(bf16[1,2,64,8,128]{4,3,2,1,0:T(8,128)(2,1)S(1)} %get-tuple-element.28), channel_id=1, source_target_pairs={{0,2},{1,3},{2,0},{3,1},{4,6},{5,7},{6,4},{7,5},{8,10},{9,11},{10,... | collective-permute-start | bytes 786440 | tf_op jit(solution)/shard_map/ppermute | solution.py:27
  17.0 25.0 %collective-permute-start.6 = (bf16[1,2,64,8,128]{4,3,2,1,0:T(8,128)(2,1)S(1)}, bf16[1,2,64,8,128]{4,3,2,1,0:T(8,128)(2,1)S(1)}, u32[]{:S(2)}, u32[]{:S(2)}) collective-permute-start(bf16[1,2,64,8,128]{4,3,2,1,0:T(8,128)(2,1)S(1)} %get-tuple-element.29), channel_id=1, source_target_pairs={{0,3},{1,2},{2,1},{3,0},{4,7},{5,6},{6,5},{7,4},{8,11},{9,10},{10,... | collective-permute-start | bytes 786440 | tf_op jit(solution)/shard_map/ppermute | solution.py:27
  19.4 20.5 %collective-permute-start.7 = (bf16[2,256,128]{2,1,0:T(8,128)(2,1)S(1)}, bf16[2,256,128]{2,1,0:T(8,128)(2,1)S(1)}, u32[]{:S(2)}, u32[]{:S(2)}) collective-permute-start(bf16[2,256,128]{2,1,0:T(8,128)(2,1)S(1)} %pad_maximum_fusion.2.refs_6_), channel_id=1, source_target_pairs={{0,8},{4,12},{8,16},{12,20},{16,24},{20,28},{1,9},{5,13},{9,17},{1... | collective-permute-start | bytes 393224 | tf_op jit(solution)/shard_map/ppermute | solution.py:22
  27.4 14.5 %collective-permute-start.8 = (bf16[2,256,128]{2,1,0:T(8,128)(2,1)S(1)}, bf16[2,256,128]{2,1,0:T(8,128)(2,1)S(1)}, u32[]{:S(2)}, u32[]{:S(2)}) collective-permute-start(bf16[2,256,128]{2,1,0:T(8,128)(2,1)S(1)} %pad_maximum_fusion.2.refs_6_), channel_id=1, source_target_pairs={{0,4},{4,8},{8,12},{12,16},{16,20},{20,24},{24,28},{1,5},{5,9},{9,... | collective-permute-start | bytes 393224 | tf_op jit(solution)/shard_map/ppermute | solution.py:22
  37.9 15.8 %collective-permute-start.14 = (bf16[2,256,128]{2,1,0:T(8,128)(2,1)S(1)}, bf16[2,256,128]{2,1,0:T(8,128)(2,1)S(1)}, u32[]{:S(2)}, u32[]{:S(2)}) collective-permute-start(bf16[2,256,128]{2,1,0:T(8,128)(2,1)S(1)} %get-tuple-element.38), channel_id=1, source_target_pairs={{8,0},{12,4},{16,8},{20,12},{24,16},{28,20},{9,1},{13,5},{17,9},{2... | collective-permute-start | bytes 393224 | tf_op jit(solution)/shard_map/ppermute | solution.py:22
  39.9 15.1 %collective-permute-start.15 = (bf16[2,256,128]{2,1,0:T(8,128)(2,1)S(1)}, bf16[2,256,128]{2,1,0:T(8,128)(2,1)S(1)}, u32[]{:S(2)}, u32[]{:S(2)}) collective-permute-start(bf16[2,256,128]{2,1,0:T(8,128)(2,1)S(1)} %get-tuple-element.39), channel_id=1, source_target_pairs={{4,0},{8,4},{12,8},{16,12},{20,16},{24,20},{28,24},{5,1},{9,5},{13... | collective-permute-start | bytes 393224 | tf_op jit(solution)/shard_map/ppermute | solution.py:22
  49.3 14.0 %collective-permute-start.16 = (bf16[2,256,128]{2,1,0:T(8,128)(2,1)S(1)}, bf16[2,256,128]{2,1,0:T(8,128)(2,1)S(1)}, u32[]{:S(2)}, u32[]{:S(2)}) collective-permute-start(bf16[2,256,128]{2,1,0:T(8,128)(2,1)S(1)} %get-tuple-element.41), channel_id=1, source_target_pairs={{8,0},{12,4},{16,8},{20,12},{24,16},{28,20},{9,1},{13,5},{17,9},{2... | collective-permute-start | bytes 393224 | tf_op jit(solution)/shard_map/ppermute | solution.py:22
  51.2 13.5 %collective-permute-start.17 = (bf16[2,256,128]{2,1,0:T(8,128)(2,1)S(1)}, bf16[2,256,128]{2,1,0:T(8,128)(2,1)S(1)}, u32[]{:S(2)}, u32[]{:S(2)}) collective-permute-start(bf16[2,256,128]{2,1,0:T(8,128)(2,1)S(1)} %get-tuple-element.42), channel_id=1, source_target_pairs={{4,0},{8,4},{12,8},{16,12},{20,16},{24,20},{28,24},{5,1},{9,5},{13... | collective-permute-start | bytes 393224 | tf_op jit(solution)/shard_map/ppermute | solution.py:22
  53.2 18.4 %collective-permute-start.9 = (bf16[2,64,8,128]{3,2,1,0:T(8,128)(2,1)S(1)}, bf16[2,64,8,128]{3,2,1,0:T(8,128)(2,1)S(1)}, u32[]{:S(2)}, u32[]{:S(2)}) collective-permute-start(bf16[2,64,8,128]{3,2,1,0:T(8,128)(2,1)S(1)} %pad_maximum_fusion), channel_id=1, source_target_pairs={{0,1},{1,0},{2,3},{3,2},{4,5},{5,4},{6,7},{7,6},{8,9},{9,8},{10,11... | collective-permute-start | bytes 786440 | tf_op jit(solution)/shard_map/ppermute | solution.py:27
  53.7 14.1 %collective-permute-start.12 = (bf16[1,64,8,128]{3,2,1,0:T(8,128)(2,1)S(1)}, bf16[1,64,8,128]{3,2,1,0:T(8,128)(2,1)S(1)}, u32[]{:S(2)}, u32[]{:S(2)}) collective-permute-start(bf16[1,64,8,128]{3,2,1,0:T(8,128)(2,1)S(1)} %get-tuple-element.35), channel_id=1, source_target_pairs={{0,2},{1,3},{2,0},{3,1},{4,6},{5,7},{6,4},{7,5},{8,10},{9,11},{10,... | collective-permute-start | bytes 393224 | tf_op jit(solution)/shard_map/ppermute | solution.py:27
  54.9 12.9 %collective-permute-start.13 = (bf16[1,64,8,128]{3,2,1,0:T(8,128)(2,1)S(1)}, bf16[1,64,8,128]{3,2,1,0:T(8,128)(2,1)S(1)}, u32[]{:S(2)}, u32[]{:S(2)}) collective-permute-start(bf16[1,64,8,128]{3,2,1,0:T(8,128)(2,1)S(1)} %get-tuple-element.36), channel_id=1, source_target_pairs={{0,3},{1,2},{2,1},{3,0},{4,7},{5,6},{6,5},{7,4},{8,11},{9,10},{10,... | collective-permute-start | bytes 393224 | tf_op jit(solution)/shard_map/ppermute | solution.py:27
  63.3 4.6 %collective-permute-start.10 = (bf16[1,64,8,128]{3,2,1,0:T(8,128)(2,1)S(1)}, bf16[1,64,8,128]{3,2,1,0:T(8,128)(2,1)S(1)}, u32[]{:S(2)}, u32[]{:S(2)}) collective-permute-start(bf16[1,64,8,128]{3,2,1,0:T(8,128)(2,1)S(1)} %get-tuple-element.33), channel_id=1, source_target_pairs={{0,2},{1,3},{2,0},{3,1},{4,6},{5,7},{6,4},{7,5},{8,10},{9,11},{10,... | collective-permute-start | bytes 393224 | tf_op jit(solution)/shard_map/ppermute | solution.py:27
  64.7 6.9 %collective-permute-start.11 = (bf16[1,64,8,128]{3,2,1,0:T(8,128)(2,1)S(1)}, bf16[1,64,8,128]{3,2,1,0:T(8,128)(2,1)S(1)}, u32[]{:S(2)}, u32[]{:S(2)}) collective-permute-start(bf16[1,64,8,128]{3,2,1,0:T(8,128)(2,1)S(1)} %get-tuple-element.34), channel_id=1, source_target_pairs={{0,3},{1,2},{2,1},{3,0},{4,7},{5,6},{6,5},{7,4},{8,11},{9,10},{10,... | collective-permute-start | bytes 393224 | tf_op jit(solution)/shard_map/ppermute | solution.py:27

commit v3 on v2

--- a/solution.py
+++ b/solution.py
@@ -18,7 +18,7 @@
 
 def shifted(value, by):
     peers = lax.axis_size(SEQ)
-    pairs = [(i, i + by) for i in range(peers) if 0 <= i + by < peers]
+    pairs = [(i, (i + by) % peers) for i in range(peers)]
     return lax.ppermute(value, SEQ, pairs)
 
 
@@ -27,68 +27,146 @@
     return lax.ppermute(value, "head", [(i, i ^ distance) for i in range(peers)])
 
 
-def pack_kernel(parts, q_ref, do_ref, *refs):
-    outs, sem = refs[:-1], refs[-1]
+def in_hbm(value):
+    return pltpu.with_memory_space_constraint(value, pltpu.HBM)
+
+
+def pack_copies(parts, sources, outs, sem, kv_heads):
     me = lax.axis_index("head")
-    kv_heads = q_ref.shape[1] // lax.axis_size("head")
     copies = []
     for out, part in zip(outs, parts):
         for n, (kv, distance) in enumerate(part):
             place = (me ^ distance) * kv_heads + kv
-            for which, source in enumerate((q_ref, do_ref)):
+            for which, source in enumerate(sources):
                 copies.append(
                     pltpu.make_async_copy(source.at[:, place], out.at[n, which], sem.at[len(copies)])
                 )
+    return copies
+
+
+def pack_kernel(parts, kv_heads, q_ref, do_ref, *refs):
+    copies = pack_copies(parts, (q_ref, do_ref), refs[:-1], refs[-1], kv_heads)
     for copy in copies:
         copy.start()
     for copy in copies:
         copy.wait()
 
 
-def pack(queries, grad_out, parts):
+def first_kernel(parts, kv_heads, key_ref, value_ref, q_ref, do_ref, *refs):
+    own_refs, outs = refs[:kv_heads], refs[kv_heads:-4]
+    narrow, wide, own_sem, sem = refs[-4:]
+    loads = [
+        pltpu.make_async_copy(source, narrow.at[which], own_sem.at[which])
+        for which, source in enumerate((key_ref, value_ref))
+    ]
+    copies = pack_copies(parts, (q_ref, do_ref), outs, sem, kv_heads)
+    for copy in loads + copies:
+        copy.start()
+    tok_rows = own_refs[0].shape[1]
+    for which, load in enumerate(loads):
+        load.wait()
+        wide[which] = narrow[which].astype(jnp.float32)
+        for kv in range(kv_heads):
+            rows = wide[which, pl.ds(kv, tok_rows, stride=kv_heads), :]
+            own_refs[kv][which] = rows.astype(own_refs[kv].dtype)
+    for copy in copies:
+        copy.wait()
+
+
+def pack(queries, grad_out, parts, kv_heads):
     part_rows, _, group, width = queries.shape
     return pl.pallas_call(
-        functools.partial(pack_kernel, parts),
+        functools.partial(pack_kernel, parts, kv_heads),
         in_specs=[HBM, HBM],
         out_specs=[VMEM] * len(parts),
         out_shape=[
-            jax.ShapeDtypeStruct((len(part), 2, part_rows, group, width), queries.dtype)
-            for part in parts
+            pltpu.VMEM((len(part), 2, part_rows, group, width), queries.dtype) for part in parts
         ],
         scratch_shapes=[pltpu.SemaphoreType.DMA((2 * sum(len(part) for part in parts),))],
         compiler_params=pltpu.CompilerParams(vmem_limit_bytes=16 * 2**20),
         name="pack",
-    )(queries, grad_out)
-
-
-def unpack_kernel(parts, *refs):
-    values, out_ref, sem = refs[:-2], refs[-2], refs[-1]
+    )(in_hbm(queries), in_hbm(grad_out))
+
+
+def pack_first(keys, values, queries, grad_out, parts):
+    tok_rows, kv_heads, width = keys.shape
+    part_rows, _, group, _ = queries.shape
+    outs = pl.pallas_call(
+        functools.partial(first_kernel, parts, kv_heads),
+        in_specs=[HBM] * 4,
+        out_specs=[VMEM] * (len(parts) + kv_heads),
+        out_shape=[pltpu.VMEM((2, tok_rows, width), keys.dtype)] * kv_heads
+        + [pltpu.VMEM((len(part), 2, part_rows, group, width), queries.dtype) for part in parts],
+        scratch_shapes=[
+            pltpu.VMEM((2, tok_rows * kv_heads, width), keys.dtype),
+            pltpu.VMEM((2, tok_rows * kv_heads, width), jnp.float32),
+            pltpu.SemaphoreType.DMA((2,)),
+            pltpu.SemaphoreType.DMA((2 * sum(len(part) for part in parts),)),
+        ],
+        compiler_params=pltpu.CompilerParams(vmem_limit_bytes=16 * 2**20),
+        name="first",
+    )(
+        in_hbm(keys.reshape(tok_rows * kv_heads, width)),
+        in_hbm(values.reshape(tok_rows * kv_heads, width)),
+        in_hbm(queries),
+        in_hbm(grad_out),
+    )
+    return outs[:kv_heads], outs[kv_heads:]
+
+
+def finish_kernel(parts, heads, *refs):
+    values, totals = refs[: len(parts)], refs[len(parts) : len(parts) + 3 * heads]
+    dq_ref, dk_ref, dv_ref, wide, narrow, sem = refs[len(parts) + 3 * heads :]
     me = lax.axis_index("head")
-    kv_heads = out_ref.shape[1] // lax.axis_size("head")
     copies = []
     for value, part in zip(values, parts):
         for n, (kv, distance) in enumerate(part):
-            place = (me ^ distance) * kv_heads + kv
+            place = (me ^ distance) * heads + kv
             copies.append(
-                pltpu.make_async_copy(value.at[n], out_ref.at[:, place], sem.at[len(copies)])
+                pltpu.make_async_copy(value.at[n], dq_ref.at[:, place], sem.at[len(copies)])
             )
     for copy in copies:
         copy.start()
+    tok_rows = totals[0].shape[1]
+    for which, out in enumerate((dk_ref, dv_ref)):
+        for kv in range(heads):
+            own, far, near = totals[3 * kv : 3 * kv + 3]
+            total = own[which] + far[which].astype(jnp.float32) + near[which].astype(jnp.float32)
+            wide[which, pl.ds(kv, tok_rows, stride=heads), :] = total
+        narrow[which] = wide[which].astype(narrow.dtype)
+        copies.append(pltpu.make_async_copy(narrow.at[which], out, sem.at[len(copies)]))
+        copies[-1].start()
     for copy in copies:
         copy.wait()
 
 
-def unpack(values, parts, places):
+def finish(values, parts, totals):
     _, part_rows, group, width = values[0].shape
-    return pl.pallas_call(
-        functools.partial(unpack_kernel, parts),
-        in_specs=[VMEM] * len(values),
-        out_specs=HBM,
-        out_shape=jax.ShapeDtypeStruct((part_rows, places, group, width), values[0].dtype),
-        scratch_shapes=[pltpu.SemaphoreType.DMA((sum(len(part) for part in parts),))],
+    heads = len(totals)
+    tok_rows = totals[0][0].shape[1]
+    places = sum(len(part) for part in parts)
+    dq, dk, dv = pl.pallas_call(
+        functools.partial(finish_kernel, parts, heads),
+        in_specs=[VMEM] * (len(values) + 3 * heads),
+        out_specs=[HBM] * 3,
+        out_shape=[
+            jax.ShapeDtypeStruct((part_rows, places, group, width), jnp.bfloat16),
+            jax.ShapeDtypeStruct((tok_rows * heads, width), jnp.bfloat16),
+            jax.ShapeDtypeStruct((tok_rows * heads, width), jnp.bfloat16),
+        ],
+        scratch_shapes=[
+            pltpu.VMEM((2, tok_rows * heads, width), jnp.float32),
+            pltpu.VMEM((2, tok_rows * heads, width), jnp.bfloat16),
+            pltpu.SemaphoreType.DMA((places + 2,)),
+        ],
         compiler_params=pltpu.CompilerParams(vmem_limit_bytes=16 * 2**20),
-        name="unpack",
-    )(*values)
+        name="finish",
+    )(*values, *(term for total in totals for term in total))
+    return (
+        dq.reshape(part_rows, places * group, width),
+        dk.reshape(tok_rows, heads, width),
+        dv.reshape(tok_rows, heads, width),
+    )
 
 
 def grads_kernel(where, *refs):
@@ -202,12 +280,15 @@
     far_cores = list(range(2, peers))
     all_kv = list(range(kv_heads))
 
-    first = pack(queries, grad_out, [[(0, d)] for d in far_cores])
+    own, first = pack_first(
+        key_vector_rows, value_vector_rows, queries, grad_out, [[(0, d)] for d in far_cores]
+    )
     rest = pack(
         queries,
         grad_out,
         [[(kv, 0) for kv in all_kv], [(kv, 1) for kv in all_kv]]
         + [[(kv, d)] for kv in all_kv[1:] for d in far_cores],
+        kv_heads,
     )
     sent = [first] + [rest[2 + n * len(far_cores) :][: len(far_cores)] for n in range(kv_heads - 1)]
     crossed, windows = [], []
@@ -216,13 +297,12 @@
         for value, d in zip(sent[kv], far_cores):
             values.append(swapped(value, d))
         crossed.append(values)
-        own = jnp.stack([key_vector_rows[:, kv], value_vector_rows[:, kv]], axis=0)
-        far = shifted(own, 2)
-        near = shifted(own, 1)
-        windows.append((far, near, own))
+        far = shifted(own[kv], 2)
+        near = shifted(own[kv], 1)
+        windows.append((far, near, own[kv]))
     here = rest[0]
     partner = swapped(rest[1], 1)
-    dq_here, dq_partner, dq_crossed, dkeys, dvalues = [], [], [], [], []
+    dq_here, dq_partner, dq_crossed, totals = [], [], [], []
     for kv in all_kv:
         dq, (dfar, dnear, down) = group_grads(
             [here, partner] + crossed[kv], [kv, kv] + [0] * len(far_cores), *windows[kv]
@@ -235,20 +315,12 @@
         for value, d in zip(dq[2:], far_cores):
             values.append(swapped(value, d))
         dq_crossed.append(values)
-        total = down + dfar.astype(jnp.float32) + dnear.astype(jnp.float32)
-        total = total.astype(jnp.bfloat16)
-        dkeys.append(total[0])
-        dvalues.append(total[1])
+        totals.append((down, dfar, dnear))
     dq_partner = swapped(jnp.concatenate(dq_partner, axis=0), 1)
     values = dq_here + [dq_partner] + sum(dq_crossed, [])
     parts = [[(kv, 0)] for kv in all_kv] + [[(kv, 1) for kv in all_kv]]
     parts += [[(kv, d)] for kv in all_kv for d in far_cores]
-    query_grads = unpack(values, parts, places)
-    return (
-        query_grads.reshape(part_rows, heads, width),
-        jnp.stack(dkeys, axis=1),
-        jnp.stack(dvalues, axis=1),
-    )
+    return finish(values, parts, totals)
 
 
 def solution(mesh):

time: 73 us -> 58.8 us (0.81)
  the two profiles are of different devices: /device:TPU:25 before, /device:TPU:0 now
where the time goes in v3:
time: 58.8 us; the launch traced here: 58.4 us
  starting transfers between devices  20 us (34%)
  waiting for transfers between devices  19.2 us (33%)
  Pallas kernels  18.6 us (32%)
  between operations  0.69 us (1%)
    ppermute x8, waiting for transfers between devices, shifted(): return lax.ppermute(value, SEQ, pairs)  15.4 us
    pallas_call x2, Pallas kernels, group_grads(): pl.pallas_call(functools.partial(grads_kernel, where), in_specs=[VMEM] *...  14.6 us
    ppermute x8, starting transfers between devices, shifted(): return lax.ppermute(value, SEQ, pairs)  10.5 us
    ppermute x10, starting transfers between devices, swapped(): lax.ppermute(value, 'head', [(i, i ^ distance) for i in range(peers)])  9.52 us
    ppermute x10, waiting for transfers between devices, swapped(): lax.ppermute(value, 'head', [(i, i ^ distance) for i in range(peers)])  3.74 us
    pallas_call x1, Pallas kernels, pack(): pl.pallas_call(functools.partial(pack_kernel, parts, kv_heads), in_specs=...  1.6 us
    pallas_call x1, Pallas kernels, pack_first(): pl.pallas_call(functools.partial(first_kernel, parts, kv_heads), in_specs...  1.27 us
  transfers between devices with their start and end apart: 18, of which 8 were waited for; matrix products, arithmetic and copies ran while one was open for 0% of the time, Pallas kernels for 27%

profile of v3, /device:TPU:0, one launch (start us, length us, event | category | flops | bytes accessed | tf_op | source)
XLA Modules:
  0.0 58.4 jit_solution(16619515156913919370)
XLA Ops:
  0.6 1.6 %pack.1 = (bf16[2,2,64,8,128]{4,3,2,1,0:T(8,128)(2,1)S(1)}, bf16[2,2,64,8,128]{4,3,2,1,0:T(8,128)(2,1)S(1)}, bf16[1,2,64,8,128]{4,3,2,1,0:T(8,128)(2,1)S(1)}, bf16[1,2,64,8,128]{4,3,2,1,0:T(8,128)(2,1)S(1)}) custom-call(bf16[64,8,8,128]{3,2,1,0:T(8,128)(2,1)} %bitcast.7, bf16[64,8,8,128]{3,2,1,0:T(8,128)(2,1)} %bitcast.9), custom_call_target="tpu_custom_call" | custom-call | tf_op jit(solution)/shard_map/pack/pallas_call | solution.py:78
  2.2 0.6 collective-permute-start
  2.8 2.6 %collective-permute-start.5 = (bf16[1,2,64,8,128]{4,3,2,1,0:T(8,128)(2,1)S(1)}, bf16[1,2,64,8,128]{4,3,2,1,0:T(8,128)(2,1)S(1)}, u32[]{:S(2)}, u32[]{:S(2)}) collective-permute-start(bf16[1,2,64,8,128]{4,3,2,1,0:T(8,128)(2,1)S(1)} %get-tuple-element.34), channel_id=1, source_target_pairs={{0,2},{1,3},{2,0},{3,1},{4,6},{5,7},{6,4},{7,5},{8,10},{9,11},{10,... | collective-permute-start | bytes 786440 | tf_op jit(solution)/shard_map/ppermute | solution.py:27
  5.3 0.0 collective-permute-start.6
  5.4 1.3 %first.1 = (bf16[2,256,128]{2,1,0:T(8,128)(2,1)S(1)}, bf16[2,256,128]{2,1,0:T(8,128)(2,1)S(1)}, bf16[1,2,64,8,128]{4,3,2,1,0:T(8,128)(2,1)S(1)}, bf16[1,2,64,8,128]{4,3,2,1,0:T(8,128)(2,1)S(1)}) custom-call(bf16[512,128]{1,0:T(8,128)(2,1)} %bitcast.11, bf16[512,128]{1,0:T(8,128)(2,1)} %bitcast.12, bf16[64,8,8,128]{3,2,1,0:T(8,128)(2,1)} %bitcast.8, ...), custom_call_target="tpu_custom_call" | custom-call | tf_op jit(solution)/shard_map/first/pallas_call | solution.py:94
  6.7 1.9 %collective-permute-start.8 = (bf16[2,256,128]{2,1,0:T(8,128)(2,1)S(1)}, bf16[2,256,128]{2,1,0:T(8,128)(2,1)S(1)}, u32[]{:S(2)}, u32[]{:S(2)}) collective-permute-start(bf16[2,256,128]{2,1,0:T(8,128)(2,1)S(1)} %get-tuple-element.36.refs_6_), channel_id=1, source_target_pairs={{0,4},{4,8},{8,12},{12,16},{16,20},{20,24},{24,28},{28,0},{1,5},{5... | collective-permute-start | bytes 393224 | tf_op jit(solution)/shard_map/ppermute | solution.py:22
  8.5 2.6 %collective-permute-start.7 = (bf16[2,256,128]{2,1,0:T(8,128)(2,1)S(1)}, bf16[2,256,128]{2,1,0:T(8,128)(2,1)S(1)}, u32[]{:S(2)}, u32[]{:S(2)}) collective-permute-start(bf16[2,256,128]{2,1,0:T(8,128)(2,1)S(1)} %get-tuple-element.36.refs_6_), channel_id=1, source_target_pairs={{0,8},{4,12},{8,16},{12,20},{16,24},{20,28},{24,0},{28,4},{1,9},{5... | collective-permute-start | bytes 393224 | tf_op jit(solution)/shard_map/ppermute | solution.py:22
  11.1 4.8 %collective-permute-done.8.refs_5_ = bf16[2,256,128]{2,1,0:T(8,128)(2,1)S(1)} collective-permute-done((bf16[2,256,128]{2,1,0:T(8,128)(2,1)S(1)}, bf16[2,256,128]{2,1,0:T(8,128)(2,1)S(1)}, u32[]{:S(2)}, u32[]{:S(2)}) %collective-permute-start.8) | collective-permute-done | bytes 131104 | tf_op jit(solution)/shard_map/ppermute | solution.py:22
  16.0 1.7 %collective-permute-start.1 = (bf16[1,2,64,8,128]{4,3,2,1,0:T(8,128)(2,1)S(1)}, bf16[1,2,64,8,128]{4,3,2,1,0:T(8,128)(2,1)S(1)}, u32[]{:S(2)}, u32[]{:S(2)}) collective-permute-start(bf16[1,2,64,8,128]{4,3,2,1,0:T(8,128)(2,1)S(1)} %get-tuple-element.30), channel_id=1, source_target_pairs={{0,2},{1,3},{2,0},{3,1},{4,6},{5,7},{6,4},{7,5},{8,10},{9,11},{10,... | collective-permute-start | bytes 786440 | tf_op jit(solution)/shard_map/ppermute | solution.py:27
  17.6 3.5 %collective-permute-done.7.refs_4_ = bf16[2,256,128]{2,1,0:T(8,128)(2,1)S(1)} collective-permute-done((bf16[2,256,128]{2,1,0:T(8,128)(2,1)S(1)}, bf16[2,256,128]{2,1,0:T(8,128)(2,1)S(1)}, u32[]{:S(2)}, u32[]{:S(2)}) %collective-permute-start.7) | collective-permute-done | bytes 131104 | tf_op jit(solution)/shard_map/ppermute | solution.py:22
  21.2 1.1 %collective-permute-start.2 = (bf16[1,2,64,8,128]{4,3,2,1,0:T(8,128)(2,1)S(1)}, bf16[1,2,64,8,128]{4,3,2,1,0:T(8,128)(2,1)S(1)}, u32[]{:S(2)}, u32[]{:S(2)}) collective-permute-start(bf16[1,2,64,8,128]{4,3,2,1,0:T(8,128)(2,1)S(1)} %get-tuple-element.31), channel_id=1, source_target_pairs={{0,3},{1,2},{2,1},{3,0},{4,7},{5,6},{6,5},{7,4},{8,11},{9,10},{10,... | collective-permute-start | bytes 786440 | tf_op jit(solution)/shard_map/ppermute | solution.py:27
  22.3 0.0 collective-permute-done.5.refs_2_
  22.3 0.0 collective-permute-start.4
  22.3 0.0 collective-permute-done.6.refs_3_
  22.3 0.7 %collective-permute-start.3 = (bf16[2,256,128]{2,1,0:T(8,128)(2,1)S(1)}, bf16[2,256,128]{2,1,0:T(8,128)(2,1)S(1)}, u32[]{:S(2)}, u32[]{:S(2)}) collective-permute-start(bf16[2,256,128]{2,1,0:T(8,128)(2,1)S(1)} %get-tuple-element.32.refs_6_), channel_id=1, source_target_pairs={{0,8},{4,12},{8,16},{12,20},{16,24},{20,28},{24,0},{28,4},{1,9},{5... | collective-permute-start | bytes 393224 | tf_op jit(solution)/shard_map/ppermute | solution.py:22
  23.0 0.0 collective-permute-done.refs_1_
  23.0 7.3 %grads.3 = (bf16[1,64,8,128]{3,2,1,0:T(8,128)(2,1)S(1)}, bf16[1,64,8,128]{3,2,1,0:T(8,128)(2,1)S(1)}, bf16[1,64,8,128]{3,2,1,0:T(8,128)(2,1)S(1)}, bf16[1,64,8,1...) custom-call(bf16[2,2,64,8,128]{4,3,2,1,0:T(8,128)(2,1)S(1)} %get-tup, ...), custom_call_target="tpu_custom_call" | custom-call | flops 2013265920 | bytes 1572864 | tf_op jit(solution)/shard_map/grads/pallas_call | solution.py:247
  30.3 1.0 %collective-permute-start.12 = (bf16[1,64,8,128]{3,2,1,0:T(8,128)(2,1)S(1)}, bf16[1,64,8,128]{3,2,1,0:T(8,128)(2,1)S(1)}, u32[]{:S(2)}, u32[]{:S(2)}) collective-permute-start(bf16[1,64,8,128]{3,2,1,0:T(8,128)(2,1)S(1)} %get-tuple-element.42), channel_id=1, source_target_pairs={{0,2},{1,3},{2,0},{3,1},{4,6},{5,7},{6,4},{7,5},{8,10},{9,11},{10,... | collective-permute-start | bytes 393224 | tf_op jit(solution)/shard_map/ppermute | solution.py:27
  31.3 0.2 collective-permute-done.4.refs_5_
  31.5 0.7 %collective-permute-start.13 = (bf16[1,64,8,128]{3,2,1,0:T(8,128)(2,1)S(1)}, bf16[1,64,8,128]{3,2,1,0:T(8,128)(2,1)S(1)}, u32[]{:S(2)}, u32[]{:S(2)}) collective-permute-start(bf16[1,64,8,128]{3,2,1,0:T(8,128)(2,1)S(1)} %get-tuple-element.43), channel_id=1, source_target_pairs={{0,3},{1,2},{2,1},{3,0},{4,7},{5,6},{6,5},{7,4},{8,11},{9,10},{10,... | collective-permute-start | bytes 393224 | tf_op jit(solution)/shard_map/ppermute | solution.py:27
  32.2 3.5 %collective-permute-done.3.refs_4_ = bf16[2,256,128]{2,1,0:T(8,128)(2,1)S(1)} collective-permute-done((bf16[2,256,128]{2,1,0:T(8,128)(2,1)S(1)}, bf16[2,256,128]{2,1,0:T(8,128)(2,1)S(1)}, u32[]{:S(2)}, u32[]{:S(2)}) %collective-permute-start.3) | collective-permute-done | bytes 131104 | tf_op jit(solution)/shard_map/ppermute | solution.py:22
  35.7 0.0 collective-permute-start.16
  35.7 0.0 collective-permute-done.1.refs_2_
  35.7 2.9 %collective-permute-start.17 = (bf16[2,256,128]{2,1,0:T(8,128)(2,1)S(1)}, bf16[2,256,128]{2,1,0:T(8,128)(2,1)S(1)}, u32[]{:S(2)}, u32[]{:S(2)}) collective-permute-start(bf16[2,256,128]{2,1,0:T(8,128)(2,1)S(1)} %get-tuple-element.49), channel_id=1, source_target_pairs={{0,28},{4,0},{8,4},{12,8},{16,12},{20,16},{24,20},{28,24},{1,29},{... | collective-permute-start | bytes 393224 | tf_op jit(solution)/shard_map/ppermute | solution.py:22
  38.6 0.0 collective-permute-done.2.refs_3_
  38.6 7.3 %grads.2 = (bf16[1,64,8,128]{3,2,1,0:T(8,128)(2,1)S(1)}, bf16[1,64,8,128]{3,2,1,0:T(8,128)(2,1)S(1)}, bf16[1,64,8,128]{3,2,1,0:T(8,128)(2,1)S(1)}, bf16[1,64,8,1...) custom-call(bf16[2,2,64,8,128]{4,3,2,1,0:T(8,128)(2,1)S(1)} %get-tup, ...), custom_call_target="tpu_custom_call" | custom-call | flops 2013265920 | bytes 1572864 | tf_op jit(solution)/shard_map/grads/pallas_call | solution.py:247
  45.9 0.4 collective-permute-start.9
  46.3 0.0 collective-permute-done.12.refs_5_
  46.3 0.6 %collective-permute-start.10 = (bf16[1,64,8,128]{3,2,1,0:T(8,128)(2,1)S(1)}, bf16[1,64,8,128]{3,2,1,0:T(8,128)(2,1)S(1)}, u32[]{:S(2)}, u32[]{:S(2)}) collective-permute-start(bf16[1,64,8,128]{3,2,1,0:T(8,128)(2,1)S(1)} %get-tuple-element.40), channel_id=1, source_target_pairs={{0,2},{1,3},{2,0},{3,1},{4,6},{5,7},{6,4},{7,5},{8,10},{9,11},{10,... | collective-permute-start | bytes 393224 | tf_op jit(solution)/shard_map/ppermute | solution.py:27
  46.9 0.0 collective-permute-done.13.refs_6_
  46.9 1.0 %collective-permute-start.11 = (bf16[1,64,8,128]{3,2,1,0:T(8,128)(2,1)S(1)}, bf16[1,64,8,128]{3,2,1,0:T(8,128)(2,1)S(1)}, u32[]{:S(2)}, u32[]{:S(2)}) collective-permute-start(bf16[1,64,8,128]{3,2,1,0:T(8,128)(2,1)S(1)} %get-tuple-element.41), channel_id=1, source_target_pairs={{0,3},{1,2},{2,1},{3,0},{4,7},{5,6},{6,5},{7,4},{8,11},{9,10},{10,... | collective-permute-start | bytes 393224 | tf_op jit(solution)/shard_map/ppermute | solution.py:27
  47.8 0.0 collective-permute-done.16.refs_11_
  47.8 0.8 %collective-permute-start.14 = (bf16[2,256,128]{2,1,0:T(8,128)(2,1)S(1)}, bf16[2,256,128]{2,1,0:T(8,128)(2,1)S(1)}, u32[]{:S(2)}, u32[]{:S(2)}) collective-permute-start(bf16[2,256,128]{2,1,0:T(8,128)(2,1)S(1)} %get-tuple-element.45), channel_id=1, source_target_pairs={{0,24},{4,28},{8,0},{12,4},{16,8},{20,12},{24,16},{28,20},{1,25},{... | collective-permute-start | bytes 393224 | tf_op jit(solution)/shard_map/ppermute | solution.py:22
  48.7 0.0 collective-permute-done.17.refs_12_
  48.7 1.5 %collective-permute-start.15 = (bf16[2,256,128]{2,1,0:T(8,128)(2,1)S(1)}, bf16[2,256,128]{2,1,0:T(8,128)(2,1)S(1)}, u32[]{:S(2)}, u32[]{:S(2)}) collective-permute-start(bf16[2,256,128]{2,1,0:T(8,128)(2,1)S(1)} %get-tuple-element.46), channel_id=1, source_target_pairs={{0,28},{4,0},{8,4},{12,8},{16,12},{20,16},{24,20},{28,24},{1,29},{... | collective-permute-start | bytes 393224 | tf_op jit(solution)/shard_map/ppermute | solution.py:22
  50.2 2.4 %collective-permute-done.10.refs_3_ = bf16[1,64,8,128]{3,2,1,0:T(8,128)(2,1)S(1)} collective-permute-done((bf16[1,64,8,128]{3,2,1,0:T(8,128)(2,1)S(1)}, bf16[1,64,8,128]{3,2,1,0:T(8,128)(2,1)S(1)}, u32[]{:S(2)}, u32[]{:S(2)}) %collective-permute-start.10) | collective-permute-done | bytes 131104 | tf_op jit(solution)/shard_map/ppermute | solution.py:27
  52.7 1.3 %collective-permute-done.11.refs_4_ = bf16[1,64,8,128]{3,2,1,0:T(8,128)(2,1)S(1)} collective-permute-done((bf16[1,64,8,128]{3,2,1,0:T(8,128)(2,1)S(1)}, bf16[1,64,8,128]{3,2,1,0:T(8,128)(2,1)S(1)}, u32[]{:S(2)}, u32[]{:S(2)}) %collective-permute-start.11) | collective-permute-done | bytes 131104 | tf_op jit(solution)/shard_map/ppermute | solution.py:27
  53.9 2.3 %collective-permute-done.14.refs_8_ = bf16[2,256,128]{2,1,0:T(8,128)(2,1)S(1)} collective-permute-done((bf16[2,256,128]{2,1,0:T(8,128)(2,1)S(1)}, bf16[2,256,128]{2,1,0:T(8,128)(2,1)S(1)}, u32[]{:S(2)}, u32[]{:S(2)}) %collective-permute-start.14) | collective-permute-done | bytes 131104 | tf_op jit(solution)/shard_map/ppermute | solution.py:22
  56.2 1.0 %collective-permute-done.15.refs_9_ = bf16[2,256,128]{2,1,0:T(8,128)(2,1)S(1)} collective-permute-done((bf16[2,256,128]{2,1,0:T(8,128)(2,1)S(1)}, bf16[2,256,128]{2,1,0:T(8,128)(2,1)S(1)}, u32[]{:S(2)}, u32[]{:S(2)}) %collective-permute-start.15) | collective-permute-done | bytes 131104 | tf_op jit(solution)/shard_map/ppermute | solution.py:22
  57.3 0.0 collective-permute-done.9.refs_2_
  57.3 1.1 %finish.1 = (bf16[64,8,8,128]{3,2,1,0:T(8,128)(2,1)}, bf16[512,128]{1,0:T(8,128)(2,1)}, bf16[512,128]{1,0:T(8,128)(2,1)}) custom-call(bf16[1,64,8,128]{3,2,1,0:T(8,128)(2,1)S(1)} %get-tuple-element.33.refs_0_, bf16[1,64,8,128]{3,2,1,0:T(8,128)(2,1)S(1)} %get-tuple-element.37.refs_1_, bf16[2,64,8,128]{3,2,1,0:T(8,128)(2,1)S(1)} %collective-permute-done.9.refs_2_, ...), custom_call_target="tpu_custom_call" | custom-call | tf_op jit(solution)/shard_map/finish/pallas_call | solution.py:148
  (1 shorter events, 0.0 us)
Async XLA Ops:
  2.2 20.8 %collective-permute-start = (bf16[2,2,64,8,128]{4,3,2,1,0:T(8,128)(2,1)S(1)}, bf16[2,2,64,8,128]{4,3,2,1,0:T(8,128)(2,1)S(1)}, u32[]{:S(2)}, u32[]{:S(2)}) collective-permute-start(bf16[2,2,64,8,128]{4,3,2,1,0:T(8,128)(2,1)S(1)} %get-tuple-element.29), channel_id=1, source_target_pairs={{0,1},{1,0},{2,3},{3,2},{4,5},{5,4},{6,7},{7,6},{8,9},{9,8},{10,11... | collective-permute-start | bytes 1572872 | tf_op jit(solution)/shard_map/ppermute | solution.py:27
  2.8 19.5 %collective-permute-start.5 = (bf16[1,2,64,8,128]{4,3,2,1,0:T(8,128)(2,1)S(1)}, bf16[1,2,64,8,128]{4,3,2,1,0:T(8,128)(2,1)S(1)}, u32[]{:S(2)}, u32[]{:S(2)}) collective-permute-start(bf16[1,2,64,8,128]{4,3,2,1,0:T(8,128)(2,1)S(1)} %get-tuple-element.34), channel_id=1, source_target_pairs={{0,2},{1,3},{2,0},{3,1},{4,6},{5,7},{6,4},{7,5},{8,10},{9,11},{10,... | collective-permute-start | bytes 786440 | tf_op jit(solution)/shard_map/ppermute | solution.py:27
  5.3 16.9 %collective-permute-start.6 = (bf16[1,2,64,8,128]{4,3,2,1,0:T(8,128)(2,1)S(1)}, bf16[1,2,64,8,128]{4,3,2,1,0:T(8,128)(2,1)S(1)}, u32[]{:S(2)}, u32[]{:S(2)}) collective-permute-start(bf16[1,2,64,8,128]{4,3,2,1,0:T(8,128)(2,1)S(1)} %get-tuple-element.35), channel_id=1, source_target_pairs={{0,3},{1,2},{2,1},{3,0},{4,7},{5,6},{6,5},{7,4},{8,11},{9,10},{10,... | collective-permute-start | bytes 786440 | tf_op jit(solution)/shard_map/ppermute | solution.py:27
  6.7 9.3 %collective-permute-start.8 = (bf16[2,256,128]{2,1,0:T(8,128)(2,1)S(1)}, bf16[2,256,128]{2,1,0:T(8,128)(2,1)S(1)}, u32[]{:S(2)}, u32[]{:S(2)}) collective-permute-start(bf16[2,256,128]{2,1,0:T(8,128)(2,1)S(1)} %get-tuple-element.36.refs_6_), channel_id=1, source_target_pairs={{0,4},{4,8},{8,12},{12,16},{16,20},{20,24},{24,28},{28,0},{1,5},{5... | collective-permute-start | bytes 393224 | tf_op jit(solution)/shard_map/ppermute | solution.py:22
  8.5 12.6 %collective-permute-start.7 = (bf16[2,256,128]{2,1,0:T(8,128)(2,1)S(1)}, bf16[2,256,128]{2,1,0:T(8,128)(2,1)S(1)}, u32[]{:S(2)}, u32[]{:S(2)}) collective-permute-start(bf16[2,256,128]{2,1,0:T(8,128)(2,1)S(1)} %get-tuple-element.36.refs_6_), channel_id=1, source_target_pairs={{0,8},{4,12},{8,16},{12,20},{16,24},{20,28},{24,0},{28,4},{1,9},{5... | collective-permute-start | bytes 393224 | tf_op jit(solution)/shard_map/ppermute | solution.py:22
  16.0 19.7 %collective-permute-start.1 = (bf16[1,2,64,8,128]{4,3,2,1,0:T(8,128)(2,1)S(1)}, bf16[1,2,64,8,128]{4,3,2,1,0:T(8,128)(2,1)S(1)}, u32[]{:S(2)}, u32[]{:S(2)}) collective-permute-start(bf16[1,2,64,8,128]{4,3,2,1,0:T(8,128)(2,1)S(1)} %get-tuple-element.30), channel_id=1, source_target_pairs={{0,2},{1,3},{2,0},{3,1},{4,6},{5,7},{6,4},{7,5},{8,10},{9,11},{10,... | collective-permute-start | bytes 786440 | tf_op jit(solution)/shard_map/ppermute | solution.py:27
  21.2 17.4 %collective-permute-start.2 = (bf16[1,2,64,8,128]{4,3,2,1,0:T(8,128)(2,1)S(1)}, bf16[1,2,64,8,128]{4,3,2,1,0:T(8,128)(2,1)S(1)}, u32[]{:S(2)}, u32[]{:S(2)}) collective-permute-start(bf16[1,2,64,8,128]{4,3,2,1,0:T(8,128)(2,1)S(1)} %get-tuple-element.31), channel_id=1, source_target_pairs={{0,3},{1,2},{2,1},{3,0},{4,7},{5,6},{6,5},{7,4},{8,11},{9,10},{10,... | collective-permute-start | bytes 786440 | tf_op jit(solution)/shard_map/ppermute | solution.py:27
  22.3 9.2 %collective-permute-start.4 = (bf16[2,256,128]{2,1,0:T(8,128)(2,1)S(1)}, bf16[2,256,128]{2,1,0:T(8,128)(2,1)S(1)}, u32[]{:S(2)}, u32[]{:S(2)}) collective-permute-start(bf16[2,256,128]{2,1,0:T(8,128)(2,1)S(1)} %get-tuple-element.32.refs_6_), channel_id=1, source_target_pairs={{0,4},{4,8},{8,12},{12,16},{16,20},{20,24},{24,28},{28,0},{1,5},{5... | collective-permute-start | bytes 393224 | tf_op jit(solution)/shard_map/ppermute | solution.py:22
  22.3 13.4 %collective-permute-start.3 = (bf16[2,256,128]{2,1,0:T(8,128)(2,1)S(1)}, bf16[2,256,128]{2,1,0:T(8,128)(2,1)S(1)}, u32[]{:S(2)}, u32[]{:S(2)}) collective-permute-start(bf16[2,256,128]{2,1,0:T(8,128)(2,1)S(1)} %get-tuple-element.32.refs_6_), channel_id=1, source_target_pairs={{0,8},{4,12},{8,16},{12,20},{16,24},{20,28},{24,0},{28,4},{1,9},{5... | collective-permute-start | bytes 393224 | tf_op jit(solution)/shard_map/ppermute | solution.py:22
  30.3 16.0 %collective-permute-start.12 = (bf16[1,64,8,128]{3,2,1,0:T(8,128)(2,1)S(1)}, bf16[1,64,8,128]{3,2,1,0:T(8,128)(2,1)S(1)}, u32[]{:S(2)}, u32[]{:S(2)}) collective-permute-start(bf16[1,64,8,128]{3,2,1,0:T(8,128)(2,1)S(1)} %get-tuple-element.42), channel_id=1, source_target_pairs={{0,2},{1,3},{2,0},{3,1},{4,6},{5,7},{6,4},{7,5},{8,10},{9,11},{10,... | collective-permute-start | bytes 393224 | tf_op jit(solution)/shard_map/ppermute | solution.py:27
  31.5 15.4 %collective-permute-start.13 = (bf16[1,64,8,128]{3,2,1,0:T(8,128)(2,1)S(1)}, bf16[1,64,8,128]{3,2,1,0:T(8,128)(2,1)S(1)}, u32[]{:S(2)}, u32[]{:S(2)}) collective-permute-start(bf16[1,64,8,128]{3,2,1,0:T(8,128)(2,1)S(1)} %get-tuple-element.43), channel_id=1, source_target_pairs={{0,3},{1,2},{2,1},{3,0},{4,7},{5,6},{6,5},{7,4},{8,11},{9,10},{10,... | collective-permute-start | bytes 393224 | tf_op jit(solution)/shard_map/ppermute | solution.py:27
  35.7 12.2 %collective-permute-start.16 = (bf16[2,256,128]{2,1,0:T(8,128)(2,1)S(1)}, bf16[2,256,128]{2,1,0:T(8,128)(2,1)S(1)}, u32[]{:S(2)}, u32[]{:S(2)}) collective-permute-start(bf16[2,256,128]{2,1,0:T(8,128)(2,1)S(1)} %get-tuple-element.48), channel_id=1, source_target_pairs={{0,24},{4,28},{8,0},{12,4},{16,8},{20,12},{24,16},{28,20},{1,25},{... | collective-permute-start | bytes 393224 | tf_op jit(solution)/shard_map/ppermute | solution.py:22
  35.7 13.0 %collective-permute-start.17 = (bf16[2,256,128]{2,1,0:T(8,128)(2,1)S(1)}, bf16[2,256,128]{2,1,0:T(8,128)(2,1)S(1)}, u32[]{:S(2)}, u32[]{:S(2)}) collective-permute-start(bf16[2,256,128]{2,1,0:T(8,128)(2,1)S(1)} %get-tuple-element.49), channel_id=1, source_target_pairs={{0,28},{4,0},{8,4},{12,8},{16,12},{20,16},{24,20},{28,24},{1,29},{... | collective-permute-start | bytes 393224 | tf_op jit(solution)/shard_map/ppermute | solution.py:22
  45.9 11.4 %collective-permute-start.9 = (bf16[2,64,8,128]{3,2,1,0:T(8,128)(2,1)S(1)}, bf16[2,64,8,128]{3,2,1,0:T(8,128)(2,1)S(1)}, u32[]{:S(2)}, u32[]{:S(2)}) collective-permute-start(bf16[2,64,8,128]{3,2,1,0:T(8,128)(2,1)S(1)} %pad_maximum_fusion), channel_id=1, source_target_pairs={{0,1},{1,0},{2,3},{3,2},{4,5},{5,4},{6,7},{7,6},{8,9},{9,8},{10,11... | collective-permute-start | bytes 786440 | tf_op jit(solution)/shard_map/ppermute | solution.py:27
  46.3 6.4 %collective-permute-start.10 = (bf16[1,64,8,128]{3,2,1,0:T(8,128)(2,1)S(1)}, bf16[1,64,8,128]{3,2,1,0:T(8,128)(2,1)S(1)}, u32[]{:S(2)}, u32[]{:S(2)}) collective-permute-start(bf16[1,64,8,128]{3,2,1,0:T(8,128)(2,1)S(1)} %get-tuple-element.40), channel_id=1, source_target_pairs={{0,2},{1,3},{2,0},{3,1},{4,6},{5,7},{6,4},{7,5},{8,10},{9,11},{10,... | collective-permute-start | bytes 393224 | tf_op jit(solution)/shard_map/ppermute | solution.py:27
  46.9 7.1 %collective-permute-start.11 = (bf16[1,64,8,128]{3,2,1,0:T(8,128)(2,1)S(1)}, bf16[1,64,8,128]{3,2,1,0:T(8,128)(2,1)S(1)}, u32[]{:S(2)}, u32[]{:S(2)}) collective-permute-start(bf16[1,64,8,128]{3,2,1,0:T(8,128)(2,1)S(1)} %get-tuple-element.41), channel_id=1, source_target_pairs={{0,3},{1,2},{2,1},{3,0},{4,7},{5,6},{6,5},{7,4},{8,11},{9,10},{10,... | collective-permute-start | bytes 393224 | tf_op jit(solution)/shard_map/ppermute | solution.py:27
  47.8 8.4 %collective-permute-start.14 = (bf16[2,256,128]{2,1,0:T(8,128)(2,1)S(1)}, bf16[2,256,128]{2,1,0:T(8,128)(2,1)S(1)}, u32[]{:S(2)}, u32[]{:S(2)}) collective-permute-start(bf16[2,256,128]{2,1,0:T(8,128)(2,1)S(1)} %get-tuple-element.45), channel_id=1, source_target_pairs={{0,24},{4,28},{8,0},{12,4},{16,8},{20,12},{24,16},{28,20},{1,25},{... | collective-permute-start | bytes 393224 | tf_op jit(solution)/shard_map/ppermute | solution.py:22
  48.7 8.6 %collective-permute-start.15 = (bf16[2,256,128]{2,1,0:T(8,128)(2,1)S(1)}, bf16[2,256,128]{2,1,0:T(8,128)(2,1)S(1)}, u32[]{:S(2)}, u32[]{:S(2)}) collective-permute-start(bf16[2,256,128]{2,1,0:T(8,128)(2,1)S(1)} %get-tuple-element.46), channel_id=1, source_target_pairs={{0,28},{4,0},{8,4},{12,8},{16,12},{20,16},{24,20},{28,24},{1,29},{... | collective-permute-start | bytes 393224 | tf_op jit(solution)/shard_map/ppermute | solution.py:22
